TPU v7x, 256 devices: a whole 4x4x8 slice. The times are simulated.
256 devices in a mesh: dp: 32 (over z, y), fsdp: 8 (over x, core).
Axes of the slice: x: 4, y: 4, z: 8, core: 2. Of those that a mesh axis runs over, the one named last changes fastest.
Arguments:
- dec_in: bfloat16 [512, 384, 512], P(('dp', 'fsdp'))
- enc_out: bfloat16 [512, 384, 512], P(('dp', 'fsdp'))
- src_lens: int32 [512], P(('dp', 'fsdp'))
- tgt_lens: int32 [512], P(('dp', 'fsdp'))
- y_cot: bfloat16 [512, 384, 512], P(('dp', 'fsdp'))
- attn_w: bfloat16 [4096, 512], P('fsdp')
- ffn_w: bfloat16 [4096, 512], P('fsdp')
- vec_params: bfloat16 [9728], P('fsdp')
Outputs:
- output 1: bfloat16 [512, 384, 512], P(('dp', 'fsdp'))
- output 2: bfloat16 [512, 384, 512], P(('dp', 'fsdp'))
- output 3: bfloat16 [512, 384, 512], P(('dp', 'fsdp'))
- output 4: float32 [4096, 512], P('fsdp')
- output 5: float32 [4096, 512], P('fsdp')
- output 6: float32 [9728], P('fsdp')
All inputs are finite; a program needn't handle non-finite values.
Results may differ from a plain program's by a relative error of at most 0.0165577.
Values are sent between devices in bfloat16 or wider.
A program may use at most 768 MiB of HBM per device.

v0:
```python
import jax
import jax.numpy as jnp
from jax import lax
from jax.sharding import PartitionSpec as P

HEAD_DIM = 64
LN_EPS = 1e-5
MASK_FILL = -1e30


def norm_fwd(resid_in, ln_gain, ln_shift):
    row_mean = jnp.mean(resid_in, axis=-1, keepdims=True)
    centred = resid_in - row_mean
    inv_std = lax.rsqrt(jnp.mean(centred * centred, axis=-1, keepdims=True) + LN_EPS)
    normed = centred * inv_std
    return (normed * ln_gain + ln_shift).astype(jnp.bfloat16), normed, inv_std


def norm_bwd(d_out, normed, inv_std, ln_gain):
    d_norm = d_out * ln_gain
    d_resid = inv_std * (d_norm - jnp.mean(d_norm, axis=-1, keepdims=True) - normed * jnp.mean(d_norm * normed, axis=-1, keepdims=True))
    return d_resid, jnp.sum(d_out * normed, axis=(0, 1)), jnp.sum(d_out, axis=(0, 1))


def attn_fwd(q_heads, k_heads, v_heads, key_mask):
    scores = jnp.einsum('bthe,bshe->bhts', q_heads, k_heads, preferred_element_type=jnp.float32)
    scores = jnp.where(key_mask[:, None], scores, MASK_FILL)
    attn_prob = jax.nn.softmax(scores, axis=-1)
    attn_out = jnp.einsum('bhts,bshe->bthe', attn_prob.astype(jnp.bfloat16), v_heads, preferred_element_type=jnp.float32)
    return attn_out.astype(jnp.bfloat16), attn_prob


def attn_bwd(d_out, q_heads, k_heads, v_heads, attn_prob):
    d_prob = jnp.einsum('bthe,bshe->bhts', d_out, v_heads, preferred_element_type=jnp.float32)
    d_value = jnp.einsum('bhts,bthe->bshe', attn_prob.astype(jnp.bfloat16), d_out, preferred_element_type=jnp.float32)
    d_score = (attn_prob * (d_prob - jnp.sum(attn_prob * d_prob, axis=-1, keepdims=True))).astype(jnp.bfloat16)
    d_query = jnp.einsum('bhts,bshe->bthe', d_score, k_heads, preferred_element_type=jnp.float32)
    d_key = jnp.einsum('bhts,bthe->bshe', d_score, q_heads, preferred_element_type=jnp.float32)
    return d_query, d_key, d_value


def gelu_grad(up_proj):
    norm_cdf = 0.5 * (1.0 + lax.erf(up_proj * 0.7071067811865476))
    norm_pdf = 0.3989422804014327 * jnp.exp(-0.5 * up_proj * up_proj)
    return norm_cdf + up_proj * norm_pdf


def unpack_params(attn_full, ffn_full, vec_full):
    d_model = attn_full.shape[1]
    ffn_dim = ffn_full.shape[0] // 2
    vec_f = vec_full.astype(jnp.float32)
    return dict(attn_mats=attn_full.reshape(8, d_model, d_model), w_up=ffn_full[:ffn_dim], w_down=ffn_full[ffn_dim:], biases=vec_f[:15 * d_model].reshape(15, d_model), up_bias=vec_f[15 * d_model:])


def layer_forward(dec_in, enc_out, src_lens, tgt_lens, weights):
    n_batch, n_tgt, d_model = dec_in.shape
    n_src = enc_out.shape[1]
    n_heads = d_model // HEAD_DIM
    attn_mats = weights['attn_mats']
    biases = weights['biases']
    tgt_pos = jnp.arange(n_tgt)
    self_mask = (tgt_pos[None, None, :] <= tgt_pos[None, :, None]) & (tgt_pos[None, None, :] < tgt_lens[:, None, None])
    cross_mask = jnp.arange(n_src)[None, None, :] < src_lens[:, None, None]
    q_scale = jnp.array([0.125, 1.0, 1.0], jnp.float32)[:, None]
    qkv_self = jnp.einsum('btd,nde->btne', dec_in, attn_mats[0:3], preferred_element_type=jnp.float32) + biases[0:3]
    qkv_self = (qkv_self * q_scale).astype(jnp.bfloat16).reshape(n_batch, n_tgt, 3, n_heads, HEAD_DIM)
    o_self, p_self = attn_fwd(qkv_self[:, :, 0], qkv_self[:, :, 1], qkv_self[:, :, 2], self_mask)
    o_self = o_self.reshape(n_batch, n_tgt, d_model)
    resid_one = dec_in.astype(jnp.float32) + jnp.einsum('btd,de->bte', o_self, attn_mats[3], preferred_element_type=jnp.float32) + biases[3]
    h_one, normed_one, inv_one = norm_fwd(resid_one, biases[9], biases[10])
    q_cross = ((jnp.einsum('btd,de->bte', h_one, attn_mats[4], preferred_element_type=jnp.float32) + biases[4]) * 0.125).astype(jnp.bfloat16).reshape(n_batch, n_tgt, n_heads, HEAD_DIM)
    kv_cross = (jnp.einsum('bsd,nde->bsne', enc_out, attn_mats[5:7], preferred_element_type=jnp.float32) + biases[5:7]).astype(jnp.bfloat16).reshape(n_batch, n_src, 2, n_heads, HEAD_DIM)
    o_cross, p_cross = attn_fwd(q_cross, kv_cross[:, :, 0], kv_cross[:, :, 1], cross_mask)
    o_cross = o_cross.reshape(n_batch, n_tgt, d_model)
    resid_two = h_one.astype(jnp.float32) + jnp.einsum('btd,de->bte', o_cross, attn_mats[7], preferred_element_type=jnp.float32) + biases[7]
    h_two, normed_two, inv_two = norm_fwd(resid_two, biases[11], biases[12])
    up_proj = jnp.einsum('btd,fd->btf', h_two, weights['w_up'], preferred_element_type=jnp.float32) + weights['up_bias']
    gelu_out = jax.nn.gelu(up_proj, approximate=False).astype(jnp.bfloat16)
    resid_three = h_two.astype(jnp.float32) + jnp.einsum('btf,fd->btd', gelu_out, weights['w_down'], preferred_element_type=jnp.float32) + biases[8]
    y_out, normed_three, inv_three = norm_fwd(resid_three, biases[13], biases[14])
    saved_acts = dict(qkv_self=qkv_self, p_self=p_self, o_self=o_self, normed_one=normed_one, inv_one=inv_one, h_one=h_one, q_cross=q_cross, kv_cross=kv_cross, p_cross=p_cross, o_cross=o_cross, normed_two=normed_two, inv_two=inv_two, h_two=h_two, up_proj=up_proj, gelu_out=gelu_out, normed_three=normed_three, inv_three=inv_three)
    return y_out, saved_acts


def layer_backward(y_cot, dec_in, enc_out, saved_acts, weights):
    n_batch, n_tgt, d_model = dec_in.shape
    n_src = enc_out.shape[1]
    n_heads = d_model // HEAD_DIM
    attn_mats = weights['attn_mats']
    biases = weights['biases']
    d_res3, g_gain3, g_shift3 = norm_bwd(y_cot.astype(jnp.float32), saved_acts['normed_three'], saved_acts['inv_three'], biases[13])
    d_res3_b = d_res3.astype(jnp.bfloat16)
    g_down = jnp.einsum('btf,btd->fd', saved_acts['gelu_out'], d_res3_b, preferred_element_type=jnp.float32)
    d_gelu = jnp.einsum('btd,fd->btf', d_res3_b, weights['w_down'], preferred_element_type=jnp.float32)
    d_up = d_gelu * gelu_grad(saved_acts['up_proj'])
    d_up_b = d_up.astype(jnp.bfloat16)
    g_up = jnp.einsum('btf,btd->fd', d_up_b, saved_acts['h_two'], preferred_element_type=jnp.float32)
    d_h2 = d_res3 + jnp.einsum('btf,fd->btd', d_up_b, weights['w_up'], preferred_element_type=jnp.float32)
    d_res2, g_gain2, g_shift2 = norm_bwd(d_h2, saved_acts['normed_two'], saved_acts['inv_two'], biases[11])
    d_res2_b = d_res2.astype(jnp.bfloat16)
    g_out_cross = jnp.einsum('btd,bte->de', saved_acts['o_cross'], d_res2_b, preferred_element_type=jnp.float32)
    d_o_cross = jnp.einsum('bte,de->btd', d_res2_b, attn_mats[7], preferred_element_type=jnp.float32).astype(jnp.bfloat16).reshape(n_batch, n_tgt, n_heads, HEAD_DIM)
    kv_cross = saved_acts['kv_cross']
    dq_cross, dk_cross, dv_cross = attn_bwd(d_o_cross, saved_acts['q_cross'], kv_cross[:, :, 0], kv_cross[:, :, 1], saved_acts['p_cross'])
    dq_cross = dq_cross.reshape(n_batch, n_tgt, d_model) * 0.125
    dq_cross_b = dq_cross.astype(jnp.bfloat16)
    g_q_cross = jnp.einsum('btd,bte->de', saved_acts['h_one'], dq_cross_b, preferred_element_type=jnp.float32)
    d_kv = jnp.stack([dk_cross, dv_cross], axis=2).reshape(n_batch, n_src, 2, d_model)
    d_kv_b = d_kv.astype(jnp.bfloat16)
    g_kv_cross = jnp.einsum('bsd,bsne->nde', enc_out, d_kv_b, preferred_element_type=jnp.float32)
    enc_grad = jnp.einsum('bsne,nde->bsd', d_kv_b, attn_mats[5:7], preferred_element_type=jnp.float32).astype(jnp.bfloat16)
    d_h1 = d_res2 + jnp.einsum('bte,de->btd', dq_cross_b, attn_mats[4], preferred_element_type=jnp.float32)
    d_res1, g_gain1, g_shift1 = norm_bwd(d_h1, saved_acts['normed_one'], saved_acts['inv_one'], biases[9])
    d_res1_b = d_res1.astype(jnp.bfloat16)
    g_out_self = jnp.einsum('btd,bte->de', saved_acts['o_self'], d_res1_b, preferred_element_type=jnp.float32)
    d_o_self = jnp.einsum('bte,de->btd', d_res1_b, attn_mats[3], preferred_element_type=jnp.float32).astype(jnp.bfloat16).reshape(n_batch, n_tgt, n_heads, HEAD_DIM)
    qkv_self = saved_acts['qkv_self']
    dq_self, dk_self, dv_self = attn_bwd(d_o_self, qkv_self[:, :, 0], qkv_self[:, :, 1], qkv_self[:, :, 2], saved_acts['p_self'])
    d_qkv = jnp.stack([dq_self * 0.125, dk_self, dv_self], axis=2).reshape(n_batch, n_tgt, 3, d_model)
    d_qkv_b = d_qkv.astype(jnp.bfloat16)
    g_qkv = jnp.einsum('btd,btne->nde', dec_in, d_qkv_b, preferred_element_type=jnp.float32)
    dec_grad = (d_res1 + jnp.einsum('btne,nde->btd', d_qkv_b, attn_mats[0:3], preferred_element_type=jnp.float32)).astype(jnp.bfloat16)
    g_attn = jnp.concatenate([g_qkv, g_out_self[None], g_q_cross[None], g_kv_cross, g_out_cross[None]], axis=0).reshape(8 * d_model, d_model)
    g_ffn = jnp.concatenate([g_up, g_down], axis=0)
    g_vec = jnp.concatenate([jnp.sum(d_qkv, axis=(0, 1)).reshape(-1), jnp.sum(d_res1, axis=(0, 1)), jnp.sum(dq_cross, axis=(0, 1)), jnp.sum(d_kv, axis=(0, 1)).reshape(-1), jnp.sum(d_res2, axis=(0, 1)), jnp.sum(d_res3, axis=(0, 1)), g_gain1, g_shift1, g_gain2, g_shift2, g_gain3, g_shift3, jnp.sum(d_up, axis=(0, 1))])
    return dec_grad, enc_grad, g_attn, g_ffn, g_vec


def solution(mesh):
    n_fsdp = mesh.shape['fsdp']
    n_dp = mesh.shape['dp']
    batch_axes = ('dp', 'fsdp')
    act_spec = P(batch_axes, None, None)
    len_spec = P(batch_axes)
    row_spec = P('fsdp', None)
    vec_spec = P('fsdp')

    def gather_all(attn_w, ffn_w, vec_params):
        return unpack_params(lax.all_gather(attn_w, 'fsdp', axis=0, tiled=True), lax.all_gather(ffn_w, 'fsdp', axis=0, tiled=True), lax.all_gather(vec_params, 'fsdp', axis=0, tiled=True))

    def device_step(dec_in, enc_out, src_lens, tgt_lens, y_cot, attn_w, ffn_w, vec_params):
        y_out, saved_acts = layer_forward(dec_in, enc_out, src_lens, tgt_lens, gather_all(attn_w, ffn_w, vec_params))
        attn_keep, ffn_keep, vec_keep, y_out = lax.optimization_barrier((attn_w, ffn_w, vec_params, y_out))
        dec_grad, enc_grad, g_attn, g_ffn, g_vec = layer_backward(y_cot, dec_in, enc_out, saved_acts, gather_all(attn_keep, ffn_keep, vec_keep))
        grad_scale = 1.0 / (dec_in.shape[0] * dec_in.shape[1] * n_fsdp * n_dp)
        grad_shards = [lax.psum(lax.psum_scatter(full_grad * grad_scale, 'fsdp', scatter_dimension=0, tiled=True), 'dp') for full_grad in (g_attn, g_ffn, g_vec)]
        return y_out, dec_grad, enc_grad, grad_shards[0], grad_shards[1], grad_shards[2]

    return jax.shard_map(device_step, mesh=mesh, in_specs=(act_spec, act_spec, len_spec, len_spec, act_spec, row_spec, row_spec, vec_spec), out_specs=(act_spec, act_spec, act_spec, row_spec, row_spec, vec_spec), check_vma=False)
```

profile of v0, /device:TPU:2, one launch (start us, length us, event | category | flops | bytes accessed | tf_op | source)
XLA Modules:
  0.0 520.8 jit_solution(11636195325914220892)
XLA Ops:
  11.6 23.3 %all-reduce = bf16[9728]{0:T(1024)(128)(2,1)S(1)} all-reduce(bf16[9728]{0:T(1024)(128)(2,1)S(1)} %dynamic-update-slice), channel_id=1, replica_groups=mesh['dp'=32,'fsdp'=8] {'fsdp'}, use_global_device_ids=true, to_apply=%add | all-reduce | flops 9728 | bytes 38912
  36.7 9.5 %all-gather.5.cloned.1.call-done = bf16[4096,512]{1,0:T(8,128)(2,1)} async-done(((bf16[512,512]{1,0:T(8,128)(2,1)}), bf16[4096,512]{1,0:T(8,128)(2,1)}) %all-gather.5.cloned.1.call-update) | async-done | bytes 4194320 | tf_op jit(solution)/shard_map/all_gather | solution.py:139
  57.6 5.3 %fusion.101 = (f32[2,8,384]{2,1,0:T(8,128)S(1)}, f32[2,8,384,384]{2,3,1,0:T(8,128)}) fusion(pred[2,384,384]{1,2,0:T(8,128)(4,1)S(1)} %broadcast_and_fusion, bf16[2,384,3,8,64]{1,4,3,0,2:T(8,128)(2,1)S(1)} %bitcast.239), kind=kOutput, calls=%fused_computation.198 | convolution fusion | flops 309068160 | bytes 11329536 | tf_op jit(solution)/shard_map/sub | solution.py:28
  62.9 4.7 fusion.56
  74.0 5.5 %fusion.103 = (f32[2,8,384]{2,1,0:T(8,128)S(1)}, f32[2,8,384,384]{2,3,1,0:T(8,128)}) fusion(pred[2,384]{1,0:T(4,128)(4,1)S(1)} %iota_compare_fusion.1, bf16[2,384,8,64]{1,3,2,0:T(8,128)(2,1)S(1)} %bitcast.252, bf16[2,384,2,8,64]{1,4,3,0,2:T(8,128)(2,1)S(1)} %bitcast.250), kind=kOutput, calls=%fused_computation.200 | convolution fusion | flops 309068160 | bytes 11036160 | tf_op jit(solution)/shard_map/sub | solution.py:28
  79.5 4.7 fusion.59
  86.8 5.8 %fusion.52 = (u8[384,2048]{1,0:T(8,128)(4,1)S(1)}, u8[384,2048]{1,0:T(8,128)(4,1)S(1)}, f32[2,384,2048]{2,1,0:T(8,128)S(1)}) fusion(f32[2048]{0:T(1024)S(1)} %slice.239, bf16[2,384,512]{2,1,0:T(8,128)(2,1)S(1)} %add_convert_fusion.2, bf16[4096,512]{1,0:T(8,128)(2,1)} %all-gather.7.cloned.1.call-done), kind=kOutput, calls=%fused_computation.109 | convolution fusion | flops 1631059968 | bytes 10756096 | tf_op jit(solution)/shard_map/btd,fd->btf/dot_general | solution.py:77
  92.7 14.8 %fusion.10 = bf16[2,384,2048]{2,1,0:T(8,128)(2,1)S(1)} fusion(f32[2,384,2048]{2,1,0:T(8,128)S(1)} %get-tuple-element.60, f32[2048]{0:T(1024)S(1)} %slice.239, u8[384,2048]{1,0:T(8,128)(4,1)S(1)} %get-tuple-element.15, u8[384,2048]{1,0:T(8,128)(4,1)S(1)} %get-tuple-element.14), kind=kLoop, calls=%fused_computation.17 | loop fusion | flops 111673344 | bytes 11018240 | tf_op jit(solution)/shard_map/convert_element_type | solution.py:78
  111.9 22.9 %all-reduce.1 = bf16[9728]{0:T(1024)(128)(2,1)S(1)} all-reduce(bf16[9728]{0:T(1024)(128)(2,1)S(1)} %dynamic-update-slice.1), channel_id=1, replica_groups=mesh['dp'=32,'fsdp'=8] {'fsdp'}, use_global_device_ids=true, to_apply=%add.1 | all-reduce | flops 9728 | bytes 38912
  136.7 5.9 %convolution_bitcast_fusion = f32[2048,512]{1,0:T(8,128)} fusion(bf16[2,384,2048]{2,1,0:T(8,128)(2,1)} %copy-done.23, bf16[2,384,512]{2,1,0:T(8,128)(2,1)S(1)} %copy-done.24, f32[2,384,512]{2,1,0:T(8,128)S(1)} %get-tuple-element.62, f32[2,384]{1,0:T(2,128)S(1)} %get-tuple-element.72, f32[2,384]{1,0:T(2,128)S(1)} %get-tuple-element.73, ...), kind=kOutput, calls=%fused_computation.52 | convolution fusion | flops 1614151680 | bytes 9713664 | tf_op jit(solution)/shard_map/btf,btd->fd/dot_general | solution.py:93
  145.6 6.8 %fusion.106 = (f32[2048]{0:T(1024)S(1)}, bf16[2,384,2048]{2,1,0:T(8,128)(2,1)S(1)}) fusion(f32[2,384,2048]{2,1,0:T(8,128)} %copy-done.11, f32[2048]{0:T(1024)S(1)} %slice.239, bf16[4096,512]{1,0:T(8,128)(2,1)} %all-gather.9.cloned.1.call-done, f32[2,384]{1,0:T(2,128)S(1)} %get-tuple-element.72, f32[2,384,512]{2,1,0:T(8,128)S(1)} %get-tuple-element.62, ...), kind=kOutput, calls=%fused_computation.203 | convolution fusion | flops 1633024000 | bytes 13924352 | tf_op jit(solution)/shard_map/btd,fd->btf/dot_general | solution.py:94
  156.2 4.3 maximum_multiply_fusion
  160.6 8.8 %reduce-scatter.3.cloned.1.call-start = ((), (), s32[]{:S(2)}) async-start(), calls=%async_computation.6 | async-start | bytes 9437184 | tf_op jit(solution)/shard_map/reduce_scatter | solution.py:146
  169.4 5.8 %multiply_reduce_fusion.2 = (f32[512]{0:T(512)S(1)}, f32[2,384]{1,0:T(2,128)S(1)}, f32[2,384]{1,0:T(2,128)S(1)}, f32[512]{0:T(512)S(1)}, f32[2,384,512]{2,1,0:T(8,128)S(1)}) fusion(f32[2,384,512]{2,1,0:T(8,128)} %copy-done.5, f32[2,384]{1,0:T(2,128)S(1)} %add_rsqrt_fusion.1, f32[2,384]{1,0:T(2,128)S(1)} %broadcast_multiply_fusion.9, ...), kind=kOutput, calls=%fused_computation.90 | convolution fusion | flops 1617688064 | bytes 10780672 | tf_op jit(solution)/shard_map/btf,fd->btd/dot_general | solution.py:98
  176.9 4.7 all-gather.11.cloned.1.call-done
  186.9 6.9 %fusion.30 = f32[2,8,64,384]{3,2,1,0:T(8,128)} fusion(bf16[2,384,8,64]{1,3,2,0:T(8,128)(2,1)} %bitcast.261, f32[2,8,384,384]{2,3,1,0:T(8,128)} %get-tuple-element.57, f32[2,8,384]{2,1,0:T(8,128)S(1)} %get-tuple-element.56), kind=kOutput, calls=%fused_computation.62 | convolution fusion | flops 306708480 | bytes 11821056 | tf_op jit(solution)/shard_map/bhts,bthe->bshe/dot_general | solution.py:35
  196.9 9.4 %multiply_reduce_fusion.1 = (f32[2,8,384]{2,1,0:T(8,128)S(1)}, f32[2,8,384,384]{2,3,1,0:T(8,128)}) fusion(f32[2,8,384,384]{2,3,1,0:T(8,128)} %get-tuple-element.57, f32[2,8,384]{2,1,0:T(8,128)S(1)} %get-tuple-element.56, bf16[2,384,8,64]{1,3,2,0:T(8,128)(2,1)} %bitcast.262, bf16[2,384,2,8,64]{1,4,3,0,2:T(8,128)(2,1)} %bitcast.248), kind=kOutput, calls=%fused_computation.7 | convolution fusion | flops 309061632 | bytes 20496384 | tf_op jit(solution)/shard_map/bthe,bshe->bhts/dot_general | solution.py:34
  206.2 10.3 %multiply_convert_fusion.1 = bf16[2,8,384,384]{2,3,1,0:T(8,128)(2,1)} fusion(f32[2,8,384,384]{2,3,1,0:T(8,128)} %get-tuple-element.65, f32[2,8,384]{2,1,0:T(8,128)S(1)} %get-tuple-element.64, f32[2,8,384,384]{2,3,1,0:T(8,128)} %get-tuple-element.57, f32[2,8,384]{2,1,0:T(8,128)S(1)} %get-tuple-element.56), kind=kLoop, calls=%fused_computation.6 | loop fusion | flops 9437184 | bytes 23642112 | tf_op jit(solution)/shard_map/convert_element_type | solution.py:36
  216.6 5.3 %fusion.107 = f32[2,8,64,384]{3,2,1,0:T(8,128)} fusion(bf16[2,384,8,64]{1,3,2,0:T(8,128)(2,1)S(1)} %bitcast.253, bf16[2,8,384,384]{2,3,1,0:T(8,128)(2,1)} %multiply_convert_fusion.1), kind=kOutput, calls=%fused_computation.204 | convolution fusion | flops 301989888 | bytes 7077888 | tf_op jit(solution)/shard_map/bhts,bthe->bshe/dot_general | solution.py:38
  225.0 4.8 fusion.97
  237.2 6.9 %fusion.34 = f32[2,8,64,384]{3,2,1,0:T(8,128)} fusion(bf16[2,384,8,64]{1,3,2,0:T(8,128)(2,1)} %bitcast.263, f32[2,8,384,384]{2,3,1,0:T(8,128)} %get-tuple-element.53, f32[2,8,384]{2,1,0:T(8,128)S(1)} %get-tuple-element.52), kind=kOutput, calls=%fused_computation.66 | convolution fusion | flops 306708480 | bytes 11821056 | tf_op jit(solution)/shard_map/bhts,bthe->bshe/dot_general | solution.py:35
  247.1 9.3 %multiply_reduce_fusion = (f32[2,8,384]{2,1,0:T(8,128)S(1)}, f32[2,8,384,384]{2,3,1,0:T(8,128)}) fusion(f32[2,8,384,384]{2,3,1,0:T(8,128)} %get-tuple-element.53, f32[2,8,384]{2,1,0:T(8,128)S(1)} %get-tuple-element.52, bf16[2,384,8,64]{1,3,2,0:T(8,128)(2,1)} %bitcast.264, bf16[2,384,3,8,64]{1,4,3,0,2:T(8,128)(2,1)} %bitcast.241), kind=kOutput, calls=%fused_computation.5 | convolution fusion | flops 309061632 | bytes 20496384 | tf_op jit(solution)/shard_map/bthe,bshe->bhts/dot_general | solution.py:34
  256.4 10.3 %multiply_convert_fusion = bf16[2,8,384,384]{2,3,1,0:T(8,128)(2,1)} fusion(f32[2,8,384,384]{2,3,1,0:T(8,128)} %get-tuple-element.69, f32[2,8,384]{2,1,0:T(8,128)S(1)} %get-tuple-element.68, f32[2,8,384,384]{2,3,1,0:T(8,128)} %get-tuple-element.53, f32[2,8,384]{2,1,0:T(8,128)S(1)} %get-tuple-element.52), kind=kLoop, calls=%fused_computation.4 | loop fusion | flops 9437184 | bytes 23642112 | tf_op jit(solution)/shard_map/convert_element_type | solution.py:36
  266.7 4.6 convolution_multiply_fusion
  274.5 5.6 %fusion.75 = f32[2,8,64,384]{3,2,1,0:T(8,128)} fusion(bf16[2,8,384,384]{2,3,1,0:T(8,128)(2,1)} %multiply_convert_fusion, bf16[2,384,3,8,64]{1,4,3,0,2:T(8,128)(2,1)} %bitcast.243), kind=kOutput, calls=%fused_computation.142 | convolution fusion | flops 301989888 | bytes 7077888 | tf_op jit(solution)/shard_map/bhts,bthe->bshe/dot_general | solution.py:38
  283.1 4.2 bitcast_dynamic-update-slice_fusion
  291.6 4.3 broadcast_multiply_fusion
  302.9 46.9 %reduce-scatter.3.cloned.1.call-done = f32[512,512]{1,0:T(8,128)} async-done(((f32[4096,512]{1,0:T(8,128)}), f32[512,512]{1,0:T(8,128)}) %reduce-scatter.3.cloned.1.call-update) | async-done | bytes 1048592 | tf_op jit(solution)/shard_map/reduce_scatter | solution.py:146
  349.9 24.0 %all-reduce.2 = f32[9728]{0:T(1024)S(1)} all-reduce(f32[9728]{0:T(1024)S(1)} %broadcast_multiply_fusion.1), channel_id=4, replica_groups=mesh['dp'=32,'fsdp'=8] {'fsdp'}, use_global_device_ids=true, to_apply=%region_35.36.clone | all-reduce | flops 9728 | bytes 77824
  376.8 77.1 %psum.23 = f32[1216]{0:T(1024)} all-reduce(f32[1216]{0:T(1024)S(1)} %dynamic-slice.3), channel_id=1, replica_groups=mesh['dp'=32,'fsdp'=8] {'dp'}, use_global_device_ids=true, to_apply=%region_36.37 | all-reduce | flops 1216 | bytes 9728 | tf_op jit(solution)/shard_map/psum | solution.py:146
  457.3 4.2 fusion.48
  461.5 48.6 %all-reduce.6.cloned.1.call-done = (f32[512,512]{1,0:T(8,128)}, f32[512,512]{1,0:T(8,128)}) async-done(((f32[512,512]{1,0:T(8,128)}, f32[512,512]{1,0:T(8,128)}), (f32[512,512]{1,0:T(8,128)}, f32[512,512]{1,0:T(8,128)})) %all-reduce.6.cloned.1.call-update) | async-done | bytes 2097168 | tf_op jit(solution)/shard_map/psum | solution.py:146
  (198 shorter events, 88.6 us)
Async XLA Ops:
  7.2 40.3 %copy-start = (bf16[2,384,512]{2,1,0:T(8,128)(2,1)S(1)}, bf16[2,384,512]{2,1,0:T(8,128)(2,1)}, u32[]{:S(2)}) copy-start(bf16[2,384,512]{2,1,0:T(8,128)(2,1)} %param.10) | copy-start | bytes 2359300
  7.2 39.0 %all-gather.5.cloned.1.call-start = ((), (), s32[]{:S(2)}) async-start(), calls=%async_computation.2 | async-start | bytes 4718592 | tf_op jit(solution)/shard_map/all_gather | solution.py:139
  7.9 78.9 %all-gather.7.cloned.1.call-start = ((), (), s32[]{:S(2)}) async-start(), calls=%async_computation.3 | async-start | bytes 4718592 | tf_op jit(solution)/shard_map/all_gather | solution.py:139
  8.7 136.9 %all-gather.9.cloned.1.call-start = ((), (), s32[]{:S(2)}) async-start(), calls=%async_computation.4 | async-start | bytes 4718592 | tf_op jit(solution)/shard_map/all_gather | solution.py:139
  57.5 5.3 %copy-start.10 = (bf16[2,384,3,512]{1,3,0,2:T(8,128)(2,1)}, bf16[2,384,3,512]{1,3,0,2:T(8,128)(2,1)S(1)}, u32[]{:S(2)}) copy-start(bf16[2,384,3,512]{1,3,0,2:T(8,128)(2,1)S(1)} %copy.137) | copy-start | bytes 7077892
  62.9 4.9 copy-start.29
  62.9 5.1 copy-start.42
  70.1 3.8 copy-start.22
  79.5 4.7 copy-start.27
  79.5 5.1 copy-start.30
  86.8 5.9 %copy-start.32 = (bf16[2,384,512]{2,1,0:T(8,128)(2,1)}, bf16[2,384,512]{2,1,0:T(8,128)(2,1)S(1)}, u32[]{:S(2)}) copy-start(bf16[2,384,512]{2,1,0:T(8,128)(2,1)S(1)} %add_convert_fusion.2) | copy-start | bytes 2359300
  92.7 14.8 %copy-start.11 = (f32[2,384,2048]{2,1,0:T(8,128)}, f32[2,384,2048]{2,1,0:T(8,128)S(1)}, u32[]{:S(2)}) copy-start(f32[2,384,2048]{2,1,0:T(8,128)S(1)} %get-tuple-element.60) | copy-start | bytes 18874372
  92.7 14.8 %copy-start.33 = (bf16[2,384,512]{2,1,0:T(8,128)(2,1)S(1)}, bf16[2,384,512]{2,1,0:T(8,128)(2,1)}, u32[]{:S(2)}) copy-start(bf16[2,384,512]{2,1,0:T(8,128)(2,1)} %copy-done.32) | copy-start | bytes 2359300
  92.7 14.8 %copy-start.40 = (bf16[4096,512]{1,0:T(8,128)(2,1)S(1)}, bf16[4096,512]{1,0:T(8,128)(2,1)}, u32[]{:S(2)}) copy-start(bf16[4096,512]{1,0:T(8,128)(2,1)} %all-gather.7.cloned.1.call-done) | copy-start | bytes 12582916
  111.0 70.6 %all-gather.11.cloned.1.call-start = ((), (), s32[]{:S(2)}) async-start(), calls=%async_computation.5 | async-start | bytes 4718592 | tf_op jit(solution)/shard_map/all_gather | solution.py:139
  111.6 191.3 %reduce-scatter.5.cloned.1.call-start = ((), (), s32[]{:S(2)}) async-start(), calls=%async_computation.7 | async-start | bytes 9437184 | tf_op jit(solution)/shard_map/reduce_scatter | solution.py:146
  145.6 8.5 %copy-start.34 = (bf16[2,384,512]{2,1,0:T(8,128)(2,1)S(1)}, bf16[2,384,512]{2,1,0:T(8,128)(2,1)}, u32[]{:S(2)}) copy-start(bf16[2,384,512]{2,1,0:T(8,128)(2,1)} %copy-done.32) | copy-start | bytes 2359300
  160.6 189.1 %reduce-scatter.3.cloned.1.call-start = ((), (), s32[]{:S(2)}) async-start(), calls=%async_computation.6 | async-start | bytes 9437184 | tf_op jit(solution)/shard_map/reduce_scatter | solution.py:146
  169.4 5.8 %copy-start.6 = (f32[2,384,512]{2,1,0:T(8,128)S(1)}, f32[2,384,512]{2,1,0:T(8,128)}, u32[]{:S(2)}) copy-start(f32[2,384,512]{2,1,0:T(8,128)} %copy-done.5) | copy-start | bytes 4718596
  225.0 4.8 copy-start.2
  225.0 4.8 copy-start.3
  225.0 5.1 copy-start.20
  283.1 4.2 copy-start.8
  283.1 4.2 copy-start.36
  283.1 4.9 copy-start.28
  295.9 214.2 %all-reduce.6.cloned.1.call-start = ((), (), s32[]{:S(2)}) async-start(), calls=%async_computation.8 | async-start | bytes 4194304 | tf_op jit(solution)/shard_map/psum | solution.py:146
  297.1 3.2 copy-start.19
  373.9 79.9 %copy-start.14 = (f32[2,384,1,512]{3,1,2,0:T(8,128)S(1)}, f32[2,384,1,512]{3,1,2,0:T(8,128)}, u32[]{:S(2)}) copy-start(f32[2,384,1,512]{3,1,2,0:T(8,128)} %copy.109) | copy-start | bytes 4718596
  373.9 79.9 %slice-start = ((bf16[4096,512]{1,0:T(8,128)(2,1)}), bf16[1024,512]{1,0:T(8,128)(2,1)S(1)}, s32[]{:S(2)}) async-start(bf16[4096,512]{1,0:T(8,128)(2,1)} %all-gather.11.cloned.1.call-done), calls=%async_computation.9 | async-start | bytes 2097152 | tf_op jit(solution)/shard_map/slice | solution.py:111
  453.8 3.5 copy-start.9
  453.8 3.5 copy-start.17
  453.8 3.5 copy-start.18
  (22 other events, 35.1 us)
Sparse Core Ops, SparseCore 0:
  9.8 36.3 all-gather.4
  48.1 34.3 all-gather.6
  111.1 34.4 all-gather.8
  147.3 34.3 all-gather.10
  184.0 53.6 reduce-scatter.4
  296.1 53.6 reduce-scatter.2
  353.4 156.7 all-reduce.5
where the time goes:
time: 530 us; the launch traced here: 521 us
  blocking collectives  147 us (28%)
  matrix products  128 us (24%)
  waiting for transfers between devices  115 us (22%)
  other arithmetic  57.9 us (11%)
  local copies, waits for them, and re-layouts  46.8 us (9%)
  between operations  16.7 us (3%)
  starting transfers between devices  9.02 us (2%)
    psum x1, blocking collectives, device_step(): lax.psum(lax.psum_scatter(full_grad * grad_scale, 'fsdp', scatter_dimensi...  77.1 us
    unnamed x3, blocking collectives  70.2 us
    psum x1, waiting for transfers between devices, device_step(): lax.psum(lax.psum_scatter(full_grad * grad_scale, 'fsdp', scatter_dimensi...  48.6 us
    reduce_scatter x2, waiting for transfers between devices, device_step(): lax.psum_scatter(full_grad * grad_scale, 'fsdp', scatter_dimension=0, til...  46.9 us
    convert_element_type x2, other arithmetic, attn_bwd(): (attn_prob * (d_prob - jnp.sum(attn_prob * d_prob, axis=-1, keepdims=True...  20.7 us
    dot_general x2, matrix products, attn_bwd(): jnp.einsum('bthe,bshe->bhts', d_out, v_heads, preferred_element_type=jnp....  18.6 us
    unnamed x111, local copies, waits for them, and re-layouts  15.3 us
    convert_element_type x1, other arithmetic, layer_forward(): gelu_out = jax.nn.gelu(up_proj, approximate=False).astype(jnp.bfloat16)  14.8 us
  transfers between devices with their start and end apart: 7, of which 5 were waited for; matrix products, arithmetic and copies ran while one was open for 37% of the time, Pallas kernels for 0%

commit v1 on v0

v1 whole, which is shorter than its diff:
```python
import functools
import jax
import jax.numpy as jnp
from jax import lax
from jax.experimental import pallas as pl
from jax.experimental.pallas import tpu as pltpu
from jax.sharding import PartitionSpec as P

LN_EPS = 1e-5
MASK_FILL = -1e30
BF = jnp.bfloat16
F32 = jnp.float32
ROWS = 256


def mm(a, b):
    return lax.dot_general(a, b, (((1,), (0,)), ((), ())), preferred_element_type=F32)


def mm_nt(a, b):
    return lax.dot_general(a, b, (((1,), (1,)), ((), ())), preferred_element_type=F32)


def mm_tn(a, b):
    return lax.dot_general(a, b, (((0,), (0,)), ((), ())), preferred_element_type=F32)


def layer_kernel(n_batch, n_tgt, n_src, d_model, ffn_dim, src_lens, tgt_lens, x, enc, dy, aw, fw, vec, y, dx, denc, ga, gf, gv,
                 q, k, v, o, h1, n1, i1, qc, kc, vc, oc, n2, i2, h2, gp, g, acc, dres, dresb):
    n_ffn = ffn_dim // d_model
    n_tok = n_batch * n_tgt
    n_chunks = n_tok // ROWS
    n_pairs = d_model // 128

    def rows(r):
        return pl.ds(pl.multiple_of(r * ROWS, ROWS), ROWS)

    def bias(i):
        return vec[i:i + 1, :]

    def add_vec(i, val):
        gv[pl.ds(i, 1), :] += jnp.sum(val, axis=0, keepdims=True)

    def norm(res):
        cen = res - jnp.mean(res, axis=-1, keepdims=True)
        inv = lax.rsqrt(jnp.mean(cen * cen, axis=-1, keepdims=True) + LN_EPS)
        return cen * inv, inv

    def norm_grad(d_out, normed, inv, slot):
        add_vec(slot, d_out * normed)
        add_vec(slot + 1, d_out)
        d_norm = d_out * bias(slot)
        return inv * (d_norm - jnp.mean(d_norm, axis=-1, keepdims=True) - normed * jnp.mean(d_norm * normed, axis=-1, keepdims=True))

    gv[...] = jnp.zeros_like(gv)

    def proj_self(r, _):
        s = rows(r)
        xr = x[s, :]
        er = enc[s, :]
        q[s, :] = ((mm(xr, aw[0]) + bias(0)) * 0.125).astype(BF)
        k[s, :] = (mm(xr, aw[1]) + bias(1)).astype(BF)
        v[s, :] = (mm(xr, aw[2]) + bias(2)).astype(BF)
        kc[s, :] = (mm(er, aw[5]) + bias(5)).astype(BF)
        vc[s, :] = (mm(er, aw[6]) + bias(6)).astype(BF)
        return 0

    lax.fori_loop(0, n_chunks, proj_self, 0)

    low_half = lax.broadcasted_iota(jnp.int32, (n_tgt, 128), 1) < 64

    def half(val, j):
        return jnp.where(low_half if j == 0 else ~low_half, val, jnp.zeros_like(val))

    def key_mask(b, causal):
        key_pos = lax.broadcasted_iota(jnp.int32, (n_tgt, n_src), 1)
        if causal:
            return (key_pos <= lax.broadcasted_iota(jnp.int32, (n_tgt, n_src), 0)) & (key_pos < tgt_lens[b])
        return key_pos < src_lens[b]

    def prob(qm, k2, mask):
        sc = jnp.where(mask, mm_nt(qm, k2), MASK_FILL)
        e = jnp.exp(sc - jnp.max(sc, axis=-1, keepdims=True))
        return e * (1.0 / jnp.sum(e, axis=-1, keepdims=True))

    def attn(q, k, v, o, causal):
        def step(i, _):
            b = i // n_pairs
            hp = i % n_pairs
            s = pl.ds(pl.multiple_of(b * n_tgt, n_tgt), n_tgt)
            c = pl.ds(pl.multiple_of(hp * 128, 128), 128)
            q2, k2, v2 = q[s, c], k[s, c], v[s, c]
            mask = key_mask(b, causal)
            outs = [mm(prob(half(q2, j), k2, mask).astype(BF), v2) for j in range(2)]
            o[s, c] = jnp.where(low_half, outs[0], outs[1]).astype(BF)
            return 0
        lax.fori_loop(0, n_batch * n_pairs, step, 0)

    def attn_grad(q, k, v, do, causal):
        def step(i, _):
            b = i // n_pairs
            hp = i % n_pairs
            s = pl.ds(pl.multiple_of(b * n_tgt, n_tgt), n_tgt)
            c = pl.ds(pl.multiple_of(hp * 128, 128), 128)
            q2, k2, v2, do2 = q[s, c], k[s, c], v[s, c], do[s, c]
            mask = key_mask(b, causal)
            qt, dot = q2.T, do2.T
            dq, dkt, dvt = [], [], []
            for j in range(2):
                p = prob(half(q2, j), k2, mask)
                dp = mm_nt(half(do2, j), v2)
                dvt.append(mm(dot[64 * j:64 * j + 64], p.astype(BF)))
                ds = (p * (dp - jnp.sum(p * dp, axis=-1, keepdims=True))).astype(BF)
                dq.append(mm(ds, k2))
                dkt.append(mm(qt[64 * j:64 * j + 64], ds))
            q[s, c] = (jnp.where(low_half, dq[0], dq[1]) * 0.125).astype(BF)
            k[s, c] = jnp.concatenate(dkt, axis=0).astype(BF).T
            v[s, c] = jnp.concatenate(dvt, axis=0).astype(BF).T
            return 0
        lax.fori_loop(0, n_batch * n_pairs, step, 0)

    attn(q, k, v, o, True)

    def post_self(r, _):
        s = rows(r)
        n1[s, :], i1[s, :] = norm(x[s, :].astype(F32) + mm(o[s, :], aw[3]) + bias(3))
        h = (n1[s, :] * bias(9) + bias(10)).astype(BF)
        h1[s, :] = h
        qc[s, :] = ((mm(h, aw[4]) + bias(4)) * 0.125).astype(BF)
        return 0

    lax.fori_loop(0, n_chunks, post_self, 0)
    attn(qc, kc, vc, oc, False)

    def ffn(r, _):
        s = rows(r)
        n2[s, :], i2[s, :] = norm(h1[s, :].astype(F32) + mm(oc[s, :], aw[7]) + bias(7))
        h = (n2[s, :] * bias(11) + bias(12)).astype(BF)
        h2[s, :] = h
        acc[s, :] = h.astype(F32) + bias(8)

        def up(f, _):
            u = mm_nt(h2[s, :], fw[f]) + vec[pl.ds(15 + f, 1), :]
            cdf = 0.5 * (1.0 + lax.erf(u * 0.7071067811865476))
            g_out = (u * cdf).astype(BF)
            g[f, s, :] = g_out
            gp[f, s, :] = cdf + u * (0.3989422804014327 * jnp.exp(-0.5 * u * u))
            acc[s, :] += mm(g_out, fw[n_ffn + f])
            return 0

        lax.fori_loop(0, n_ffn, up, 0)
        normed, inv = norm(acc[s, :])
        y[s, :] = (normed * bias(13) + bias(14)).astype(BF)
        d3 = norm_grad(dy[s, :].astype(F32), normed, inv, 13)
        add_vec(8, d3)
        dres[s, :] = d3
        dresb[s, :] = d3.astype(BF)
        return 0

    lax.fori_loop(0, n_chunks, ffn, 0)

    def ffn_grad(f, _):
        gf[n_ffn + f] = mm_tn(g[f], dresb[...])

        def up_grad(r, _):
            s = rows(r)
            d_up = mm_nt(dresb[s, :], fw[n_ffn + f]) * gp[f, s, :]
            add_vec(15 + f, d_up)
            d_up = d_up.astype(BF)
            g[f, s, :] = d_up
            dres[s, :] += mm(d_up, fw[f])
            return 0

        lax.fori_loop(0, n_chunks, up_grad, 0)
        gf[f] = mm_tn(g[f], h2[...])
        return 0

    lax.fori_loop(0, n_ffn, ffn_grad, 0)

    def norm2_grad(r, _):
        s = rows(r)
        d2 = norm_grad(dres[s, :], n2[s, :], i2[s, :], 11)
        add_vec(7, d2)
        dres[s, :] = d2
        d2 = d2.astype(BF)
        dresb[s, :] = d2
        h2[s, :] = mm_nt(d2, aw[7]).astype(BF)
        return 0

    lax.fori_loop(0, n_chunks, norm2_grad, 0)
    ga[7] = mm_tn(oc[...], dresb[...])
    attn_grad(qc, kc, vc, h2, False)
    ga[4] = mm_tn(h1[...], qc[...])
    ga[5] = mm_tn(enc[...], kc[...])
    ga[6] = mm_tn(enc[...], vc[...])

    def norm1_grad(r, _):
        s = rows(r)
        add_vec(4, qc[s, :].astype(F32))
        add_vec(5, kc[s, :].astype(F32))
        add_vec(6, vc[s, :].astype(F32))
        denc[s, :] = (mm_nt(kc[s, :], aw[5]) + mm_nt(vc[s, :], aw[6])).astype(BF)
        d1 = norm_grad(dres[s, :] + mm_nt(qc[s, :], aw[4]), n1[s, :], i1[s, :], 9)
        add_vec(3, d1)
        dres[s, :] = d1
        d1 = d1.astype(BF)
        dresb[s, :] = d1
        h2[s, :] = mm_nt(d1, aw[3]).astype(BF)
        return 0

    lax.fori_loop(0, n_chunks, norm1_grad, 0)
    ga[3] = mm_tn(o[...], dresb[...])
    attn_grad(q, k, v, h2, True)
    ga[0] = mm_tn(x[...], q[...])
    ga[1] = mm_tn(x[...], k[...])
    ga[2] = mm_tn(x[...], v[...])

    def last(r, _):
        s = rows(r)
        add_vec(0, q[s, :].astype(F32))
        add_vec(1, k[s, :].astype(F32))
        add_vec(2, v[s, :].astype(F32))
        dx[s, :] = (dres[s, :] + mm_nt(q[s, :], aw[0]) + mm_nt(k[s, :], aw[1]) + mm_nt(v[s, :], aw[2])).astype(BF)
        return 0

    lax.fori_loop(0, n_chunks, last, 0)


def local_layer(dec_in, enc_out, src_lens, tgt_lens, y_cot, aw, fw, vec):
    n_batch, n_tgt, d = dec_in.shape
    n_src = enc_out.shape[1]
    n_tok = n_batch * n_tgt
    ffn_dim = fw.shape[0] * d // 2
    tok = lambda dt: pltpu.VMEM((n_tok, d), dt)
    n_ffn = ffn_dim // d
    vm = pl.BlockSpec(memory_space=pltpu.VMEM)
    sm = pl.BlockSpec(memory_space=pltpu.SMEM)
    act = jax.ShapeDtypeStruct((n_tok, d), BF)
    col = pltpu.VMEM((n_tok, 1), F32)
    y, dx, denc, ga, gf, gv = pl.pallas_call(
        functools.partial(layer_kernel, n_batch, n_tgt, n_src, d, ffn_dim),
        out_shape=(act, act, act, jax.ShapeDtypeStruct(aw.shape, F32), jax.ShapeDtypeStruct(fw.shape, F32), jax.ShapeDtypeStruct(vec.shape, F32)),
        in_specs=[sm, sm] + [vm] * 6,
        out_specs=(vm,) * 6,
        scratch_shapes=[tok(BF)] * 4 + [tok(BF), tok(F32), col] + [tok(BF)] * 4 + [tok(F32), col, tok(BF),
                        pltpu.VMEM((n_ffn, n_tok, d), F32), pltpu.VMEM((n_ffn, n_tok, d), BF), tok(F32), tok(F32), tok(BF)],
        compiler_params=pltpu.CompilerParams(vmem_limit_bytes=67043328),
        cost_estimate=pl.CostEstimate(flops=24 * 10**9, bytes_accessed=30 * 2**20, transcendentals=0),
        name='layer',
    )(src_lens, tgt_lens, dec_in.reshape(n_tok, d), enc_out.reshape(n_tok, d), y_cot.reshape(n_tok, d), aw, fw, vec)
    return y.reshape(dec_in.shape), dx.reshape(dec_in.shape), denc.reshape(enc_out.shape), ga, gf, gv


def solution(mesh):
    n_fsdp = mesh.shape['fsdp']
    n_dp = mesh.shape['dp']
    batch_axes = ('dp', 'fsdp')
    act_spec = P(batch_axes, None, None)
    len_spec = P(batch_axes)
    row_spec = P('fsdp', None)
    vec_spec = P('fsdp')

    def device_step(dec_in, enc_out, src_lens, tgt_lens, y_cot, attn_w, ffn_w, vec_params):
        d = attn_w.shape[1]
        n_vec = vec_params.shape[0]
        vec_rows = -(-n_vec // d)
        vec_pad = jnp.pad(vec_params, (0, vec_rows * d - n_vec)).reshape(vec_rows, d)
        packed = lax.all_gather(jnp.concatenate([attn_w, vec_pad], axis=0), 'fsdp', axis=0)
        aw = packed[:, :d]
        vec = packed[:, d:].reshape(n_fsdp, vec_rows * d)[:, :n_vec].reshape(-1, d).astype(F32)
        fw = lax.all_gather(ffn_w, 'fsdp', axis=0)
        y, dx, denc, ga, gf, gv = local_layer(dec_in, enc_out, src_lens, tgt_lens, y_cot, aw, fw, vec)
        scale = 1.0 / (dec_in.shape[0] * dec_in.shape[1] * n_fsdp * n_dp)
        gv = lax.psum(gv.reshape(n_fsdp, n_vec), batch_axes)
        gv = lax.dynamic_index_in_dim(gv, lax.axis_index('fsdp'), 0, keepdims=False)
        ga = lax.psum_scatter(ga.reshape(-1, d), 'fsdp', scatter_dimension=0, tiled=True)
        gf = lax.psum_scatter(gf.reshape(-1, d), 'fsdp', scatter_dimension=0, tiled=True)
        ga, gf = lax.psum((ga, gf), 'dp')
        return y, dx, denc, ga * scale, gf * scale, gv * scale

    return jax.shard_map(device_step, mesh=mesh, in_specs=(act_spec, act_spec, len_spec, len_spec, act_spec, row_spec, row_spec, vec_spec), out_specs=(act_spec, act_spec, act_spec, row_spec, row_spec, vec_spec), check_vma=False)
```

time: 530 us -> 451 us (0.85)
  the two profiles are of different devices: /device:TPU:2 before, /device:TPU:8 now
where the time goes in v1:
time: 451 us; the launch traced here: 449 us
  waiting for transfers between devices  260 us (58%)
  Pallas kernels  86.5 us (19%)
  blocking collectives  76.1 us (17%)
  between operations  13.8 us (3%)
  local copies, waits for them, and re-layouts  6.8 us (2%)
  other arithmetic  5.6 us (1%)
    pallas_call x1, Pallas kernels, local_layer(): pl.pallas_call(functools.partial(layer_kernel, n_batch, n_tgt, n_src, d,...  86.5 us
    psum x1, waiting for transfers between devices, device_step(): ga, gf = lax.psum((ga, gf), 'dp')  79.6 us
    psum x1, blocking collectives, device_step(): gv = lax.psum(gv.reshape(n_fsdp, n_vec), batch_axes)  76.1 us
    reduce_scatter x1, waiting for transfers between devices, device_step(): lax.psum_scatter(gf.reshape(-1, d), 'fsdp', scatter_dimension=0, tiled=True)  57.2 us
    reduce_scatter x1, waiting for transfers between devices, device_step(): lax.psum_scatter(ga.reshape(-1, d), 'fsdp', scatter_dimension=0, tiled=True)  54.5 us
    all_gather x1, waiting for transfers between devices, device_step(): lax.all_gather(jnp.concatenate([attn_w, vec_pad], axis=0), 'fsdp', axis=0)  37.1 us
    all_gather x1, waiting for transfers between devices, device_step(): fw = lax.all_gather(ffn_w, 'fsdp', axis=0)  30.3 us
  transfers between devices with their start and end apart: 5, of which 5 were waited for; matrix products, arithmetic and copies ran while one was open for 1% of the time, Pallas kernels for 0%

profile of v1, /device:TPU:8, one launch (start us, length us, event | category | flops | bytes accessed | tf_op | source)
XLA Modules:
  0.0 449.1 jit_solution(783227192306529264)
XLA Ops:
  7.2 0.0 all-gather.8.cloned.1.call-start
  7.2 0.7 pad.4
  7.9 1.9 maximum_bitcast_fusion
  9.8 0.0 all-gather.8.cloned.1.call-update
  9.8 0.0 all-gather.6.cloned.1.call-start
  9.9 0.7 all-gather.6.cloned.1.call-update
  10.6 0.0 reduce-scatter.3.cloned.1.call-start
  10.6 37.1 %all-gather.8.cloned.1.call-done = bf16[8,515,512]{2,1,0:T(8,128)(2,1)} async-done(((bf16[1,515,512]{2,1,0:T(8,128)(2,1)}), bf16[8,515,512]{2,1,0:T(8,128)(2,1)}) %all-gather.8.cloned.1.call-update) | async-done | bytes 4218896 | tf_op jit(solution)/shard_map/all_gather | solution.py:268
  47.8 0.8 slice_bitcast_fusion
  48.6 0.7 reshape.61.vec
  49.3 4.4 slice.12.aw
  53.8 30.3 %all-gather.6.cloned.1.call-done = bf16[4096,512]{1,0:T(8,128)(2,1)} async-done(((bf16[512,512]{1,0:T(8,128)(2,1)}), bf16[4096,512]{1,0:T(8,128)(2,1)}) %all-gather.6.cloned.1.call-update) | async-done | bytes 4194320 | tf_op jit(solution)/shard_map/all_gather | solution.py:271
  84.1 86.5 %layer.1 = (bf16[768,512]{1,0:T(8,128)(2,1)}, bf16[768,512]{1,0:T(8,128)(2,1)}, bf16[768,512]{1,0:T(8,128)(2,1)}, f32[8,512,512]{2,1,0:T(8,128)}, f32[8,512,512]{2,1,0:T(8,128)}, /*index=5*/f32[19,512]{1,0:T(8,128)}) custom-call(s32[2]{0:T(128)} %src_lens.1, s32[2]{0:T(128)} %tgt_lens.1, bf16[768,512]{1,0:T(8,128)(2,1)} %bitcast.18, ...), custom_call_target="tpu_custom_call" | custom-call | flops 24000000000 | bytes 31457280 | tf_op jit(solution)/shard_map/layer/pallas_call | solution.py:240
  170.7 0.0 reduce-scatter.3.cloned.1.call-update
  170.7 0.0 reduce-scatter.5.cloned.1.call-start
  170.7 0.0 copy-start
  170.7 0.5 reduce-scatter.5.cloned.1.call-update
  171.3 0.0 all-reduce.4.cloned.1.call-start
  171.3 54.5 %reduce-scatter.3.cloned.1.call-done = f32[512,512]{1,0:T(8,128)} async-done(((f32[4096,512]{1,0:T(8,128)}), f32[512,512]{1,0:T(8,128)}) %reduce-scatter.3.cloned.1.call-update) | async-done | bytes 1048592 | tf_op jit(solution)/shard_map/reduce_scatter | solution.py:276
  225.8 57.2 %reduce-scatter.5.cloned.1.call-done = f32[512,512]{1,0:T(8,128)} async-done(((f32[4096,512]{1,0:T(8,128)}), f32[512,512]{1,0:T(8,128)}) %reduce-scatter.5.cloned.1.call-update) | async-done | bytes 1048592 | tf_op jit(solution)/shard_map/reduce_scatter | solution.py:277
  283.0 0.0 all-reduce.4.cloned.1.call-update
  283.0 0.0 copy-done
  283.0 0.1 reshape.60
  283.1 76.1 %psum.23 = f32[8,1216]{1,0:T(8,128)S(1)} all-reduce(f32[8,1216]{1,0:T(8,128)S(1)} %reshape.60), channel_id=1, replica_groups=mesh['dp'=32,'fsdp'=8] {'dp','fsdp'}, use_global_device_ids=true, to_apply=%region_4.5 | all-reduce | flops 9728 | bytes 77824 | tf_op jit(solution)/shard_map/psum | solution.py:274
  359.2 0.6 multiply_reduce_fusion
  359.9 79.6 %all-reduce.4.cloned.1.call-done = (f32[512,512]{1,0:T(8,128)}, f32[512,512]{1,0:T(8,128)}) async-done(((f32[512,512]{1,0:T(8,128)}, f32[512,512]{1,0:T(8,128)}), (f32[512,512]{1,0:T(8,128)}, f32[512,512]{1,0:T(8,128)})) %all-reduce.4.cloned.1.call-update) | async-done | bytes 2097168 | tf_op jit(solution)/shard_map/psum | solution.py:278
  439.5 3.1 broadcast_multiply_fusion
  (3 shorter events, 0.0 us)
Async XLA Ops:
  7.2 40.6 %all-gather.8.cloned.1.call-start = ((), (), s32[]{:S(2)}) async-start(), calls=%async_computation.5 | async-start | bytes 4792320 | tf_op jit(solution)/shard_map/all_gather | solution.py:268
  9.8 74.3 %all-gather.6.cloned.1.call-start = ((), (), s32[]{:S(2)}) async-start(), calls=%async_computation.4 | async-start | bytes 4718592 | tf_op jit(solution)/shard_map/all_gather | solution.py:271
  10.6 215.2 %reduce-scatter.3.cloned.1.call-start = ((), (), s32[]{:S(2)}) async-start(), calls=%async_computation.2 | async-start | bytes 9437184 | tf_op jit(solution)/shard_map/reduce_scatter | solution.py:276
  170.7 112.3 %reduce-scatter.5.cloned.1.call-start = ((), (), s32[]{:S(2)}) async-start(), calls=%async_computation.3 | async-start | bytes 9437184 | tf_op jit(solution)/shard_map/reduce_scatter | solution.py:277
  170.7 112.3 %copy-start = (f32[19,512]{1,0:T(8,128)S(1)}, f32[19,512]{1,0:T(8,128)}, u32[]{:S(2)}) copy-start(f32[19,512]{1,0:T(8,128)} %get-tuple-element.17) | copy-start | bytes 116740
  171.3 268.2 %all-reduce.4.cloned.1.call-start = ((), (), s32[]{:S(2)}) async-start(), calls=%async_computation.6 | async-start | bytes 4194304 | tf_op jit(solution)/shard_map/psum | solution.py:278
Sparse Core Ops, SparseCore 0:
  10.4 37.3 all-gather.7
  49.6 34.4 all-gather.5
  170.8 54.9 reduce-scatter.2
  228.2 54.7 reduce-scatter.4
  286.5 152.9 all-reduce.3

commit v2 on v1

--- a/solution.py
+++ b/solution.py
@@ -25,12 +25,296 @@
     return lax.dot_general(a, b, (((0,), (0,)), ((), ())), preferred_element_type=F32)
 
 
-def layer_kernel(n_batch, n_tgt, n_src, d_model, ffn_dim, src_lens, tgt_lens, x, enc, dy, aw, fw, vec, y, dx, denc, ga, gf, gv,
-                 q, k, v, o, h1, n1, i1, qc, kc, vc, oc, n2, i2, h2, gp, g, acc, dres, dresb):
+N_X = 4
+N_Y = 4
+N_Z = 8
+MESH = pl.DeviceIdType.MESH
+
+
+def layer_kernel(n_batch, n_tgt, n_src, d_model, ffn_dim, scale, src_lens, tgt_lens, x, enc, dy, attn_w, ffn_w, vec_w,
+                 y, dx, denc, attn_out, ffn_out, vec_out,
+                 aw, fw, ga, gf, gv, vec, vec_all, q, k, v, o, h1, n1, i1, qc, kc, vc, oc, n2, i2, h2, gp, g, dres, dresb,
+                 a1, a2, b1, b2, c1, c2, e1, e2, z_in, vec_pair, vec_x, vec_y, vec_z, send_sems, recv_sems):
+    acc = dres
     n_ffn = ffn_dim // d_model
     n_tok = n_batch * n_tgt
     n_chunks = n_tok // ROWS
     n_pairs = d_model // 128
+    half_rows = d_model // 2
+    y_rows = half_rows // N_Y
+    z_rows = y_rows // N_Z
+
+    dp = lax.axis_index('dp')
+    fs = lax.axis_index('fsdp')
+    my_z, my_y = dp // N_Y, dp % N_Y
+    my_x, core = fs // 2, fs % 2
+    other = 1 - core
+    sem_count = [0]
+
+    def along_x(step):
+        return (dp, (my_x + step) % N_X * 2 + core)
+
+    def along_y(step):
+        return (my_z * N_Y + (my_y + step) % N_Y, fs)
+
+    def along_z(step):
+        return ((my_z + step) % N_Z * N_Y + my_y, fs)
+
+    partner = (dp, my_x * 2 + other)
+
+    def new_sem():
+        sem_count[0] += 1
+        return sem_count[0] - 1
+
+    def remote(src, dst, sem, device):
+        return pltpu.make_async_remote_copy(src_ref=src, dst_ref=dst, send_sem=send_sems.at[sem], recv_sem=recv_sems.at[sem], device_id=device, device_id_type=MESH)
+
+    def send(src, dst, device):
+        copy = remote(src, dst, new_sem(), device)
+        copy.start()
+        return copy
+
+    barrier = pltpu.get_barrier_semaphore()
+    peers = [(dp, (fs + i) % (2 * N_X)) for i in range(1, 2 * N_X)]
+    peers += [along_y(i) for i in range(1, N_Y)] + [along_z(i) for i in range(1, N_Z)]
+    for peer in peers:
+        pl.semaphore_signal(barrier, inc=1, device_id=peer, device_id_type=MESH)
+    pl.semaphore_wait(barrier, len(peers))
+
+    class Gather:
+        def __init__(self, block, full):
+            self.block, self.full, self.copies = block, full, []
+            self.xs = [(my_x + i) % N_X for i in range(N_X)]
+
+        def go(self, src, device):
+            self.copies.append(send(src, src, device))
+            return self.copies[-1]
+
+        def start(self):
+            mine = self.full.at[fs]
+            self.up = send(self.block, mine, along_x(1))
+            self.down = send(self.block, mine, along_x(3))
+            self.across = send(self.block, mine, partner)
+            self.full[fs] = self.block[...]
+
+        def forward(self):
+            prev = self.full.at[self.xs[3] * 2 + core]
+            nxt = self.full.at[self.xs[1] * 2 + core]
+            self.up.wait_recv()
+            self.up2 = send(self.full.at[self.xs[3] * 2 + core, 0:half_rows], self.full.at[self.xs[3] * 2 + core, 0:half_rows], along_x(1))
+            self.down.wait_recv()
+            self.down2 = send(self.full.at[self.xs[1] * 2 + core, half_rows:], self.full.at[self.xs[1] * 2 + core, half_rows:], along_x(3))
+            self.go(prev, partner)
+            self.go(nxt, partner)
+
+        def spread(self):
+            self.up2.wait_recv()
+            self.go(self.full.at[self.xs[2] * 2 + core, 0:half_rows], partner)
+            self.down2.wait_recv()
+            self.go(self.full.at[self.xs[2] * 2 + core, half_rows:], partner)
+
+        def finish(self):
+            self.across.wait_recv()
+            for copy in self.copies:
+                copy.wait_recv()
+            for copy in self.copies + [self.up, self.down, self.across, self.up2, self.down2]:
+                copy.wait_send()
+
+    class Ring:
+        def __init__(self, along, pos, part, bufs, sems=None):
+            self.along, self.pos, self.part, self.bufs = along, pos, part, bufs
+
+        def start(self):
+            near, _ = self.bufs
+            far = (self.pos + 2) % 4
+            self.c = [send(self.part(far, 0), near.at[0], self.along(1)), send(self.part(far, 1), near.at[1], self.along(3))]
+
+        def relay(self):
+            near, full = self.bufs
+            nxt, prev = (self.pos + 1) % 4, (self.pos + 3) % 4
+            self.c[0].wait_recv()
+            self.part(nxt, 0)[...] += near[0]
+            self.c[1].wait_recv()
+            self.part(prev, 1)[...] += near[1]
+            self.c += [send(self.part(nxt, None), full.at[0], self.along(1)), send(self.part(prev, None), full.at[1], self.along(3))]
+
+        def finish(self):
+            _, full = self.bufs
+            self.c[2].wait_recv()
+            self.c[3].wait_recv()
+            self.part(self.pos, None)[...] += full[0] + full[1]
+            for copy in self.c:
+                copy.wait_send()
+
+    def piece(start, size, i, j):
+        if j is None:
+            return pl.ds(pl.multiple_of(start + size * i, 8), size)
+        return pl.ds(pl.multiple_of(start + size * i + size // 2 * j, 8), size // 2)
+
+    class Reduce:
+        def __init__(self, grad, pair_in, out):
+            self.grad, self.pair_in, self.out = grad, pair_in, out
+            own = lambda i, rows: grad.at[i, core, rows]
+            self.first = [Ring(along_x, my_x, lambda i, j: own(i, slice(0, half_rows) if j is None else slice(half_rows // 2 * j, half_rows // 2 * (j + 1))), (a1, a2)),
+                          Ring(along_y, my_y, lambda i, j: grad.at[:, core, piece(half_rows, y_rows, i, j)], (b1, b2))]
+            self.second = [Ring(along_y, my_y, lambda i, j: own(my_x, piece(0, y_rows, i, j)), (c1, c2)),
+                           Ring(along_x, my_x, lambda i, j: own(i, piece(half_rows + y_rows * my_y, y_rows, 0, j)), (e1, e2))]
+
+        def z_part(self, ref, h, z):
+            return ref.at[pl.ds(pl.multiple_of(half_rows * h + y_rows * my_y + z_rows * z, 8), z_rows)]
+
+        def y_part(self, h, pos):
+            return self.out.at[pl.ds(pl.multiple_of(half_rows * h + y_rows * pos, 8), y_rows)]
+
+        def r0(self):
+            self.pair = [send(self.grad.at[i, other], self.pair_in(i), partner) for i in range(N_X)]
+
+        def r1(self):
+            for i in range(N_X):
+                self.pair[i].wait_recv()
+
+                def add(j, _):
+                    s = pl.ds(pl.multiple_of(j * 128, 128), 128)
+                    self.grad[i, core, s] += self.pair_in(i)[s]
+                    return 0
+
+                lax.fori_loop(0, d_model // 128, add, 0)
+            for copy in self.pair:
+                copy.wait_send()
+            for ring in self.first:
+                ring.start()
+
+        def r2(self):
+            for ring in self.first:
+                ring.relay()
+
+        def r3(self):
+            for ring in self.first:
+                ring.finish()
+            for ring in self.second:
+                ring.start()
+
+        def r4(self):
+            for ring in self.second:
+                ring.relay()
+
+        def r5(self):
+            for ring in self.second:
+                ring.finish()
+            block = self.grad.at[my_x, core]
+            self.z = [(i, h, send(self.z_part(block, h, (my_z + i) % N_Z), z_in.at[i - 1, h], along_z(i))) for i in range(1, N_Z) for h in range(2)]
+
+        def r6(self):
+            for _, _, copy in self.z:
+                copy.wait_recv()
+            block = self.grad.at[my_x, core]
+            for h in range(2):
+                total = self.z_part(block, h, my_z)[...]
+                for i in range(1, N_Z):
+                    total += z_in[i - 1, h]
+                self.z_part(self.out, h, my_z)[...] = total * scale
+            for _, _, copy in self.z:
+                copy.wait_send()
+            self.z = [(i, h, send(self.z_part(self.out, h, my_z), self.z_part(self.out, h, my_z), along_z(i))) for i in range(1, N_Z) for h in range(2)]
+
+        def r7(self):
+            for _, _, copy in self.z:
+                copy.wait_recv()
+            for _, _, copy in self.z:
+                copy.wait_send()
+            self.c = [send(self.y_part(h, my_y), self.y_part(h, my_y), along_y(i)) for i in (1, 3) for h in range(2)]
+
+        def r8(self):
+            for copy in self.c:
+                copy.wait_recv()
+            self.c += [send(self.y_part(0, (my_y + 3) % N_Y), self.y_part(0, (my_y + 3) % N_Y), along_y(1)),
+                       send(self.y_part(1, (my_y + 1) % N_Y), self.y_part(1, (my_y + 1) % N_Y), along_y(3))]
+
+        def r9(self):
+            for copy in self.c[4:]:
+                copy.wait_recv()
+            for copy in self.c:
+                copy.wait_send()
+
+    class ReduceVec:
+        def __init__(self):
+            self.rows = vec_out.shape[0] // N_Z
+
+        def part(self, ref, z):
+            return ref.at[pl.ds(pl.multiple_of(self.rows * z, 8), self.rows)]
+
+        def swap(self, slots, pos, along):
+            return [send(slots.at[pos], slots.at[pos], along(i)) for i in range(1, 4)]
+
+        def total(self, slots, copies):
+            for copy in copies:
+                copy.wait_recv()
+            for copy in copies:
+                copy.wait_send()
+            return slots[0] + slots[1] + slots[2] + slots[3]
+
+        def r1(self):
+            for i in range(d_model // 128):
+                vec_pair[0, 32 * i:32 * i + 32] = gv[:, 128 * i:128 * i + 128]
+            self.c = [send(vec_pair.at[0], vec_pair.at[1], partner)]
+
+        def r2(self):
+            self.c[0].wait_recv()
+            vec_x[my_x] = vec_pair[0] + vec_pair[1]
+            self.c[0].wait_send()
+            self.c = self.swap(vec_x, my_x, along_x)
+
+        def r3(self):
+            vec_y[my_y] = self.total(vec_x, self.c)
+            self.c = self.swap(vec_y, my_y, along_y)
+
+        def r5(self):
+            vec_pair[0] = self.total(vec_y, self.c)
+            self.c = [send(self.part(vec_pair.at[0], (my_z + i) % N_Z), vec_z.at[i - 1], along_z(i)) for i in range(1, N_Z)]
+
+        def r6(self):
+            for copy in self.c:
+                copy.wait_recv()
+            total = self.part(vec_pair.at[0], my_z)[...]
+            for i in range(1, N_Z):
+                total += vec_z[i - 1]
+            self.part(vec_out, my_z)[...] = total * scale
+            for copy in self.c:
+                copy.wait_send()
+            self.c = [send(self.part(vec_out, my_z), self.part(vec_out, my_z), along_z(i)) for i in range(1, N_Z)]
+
+        def r7(self):
+            for copy in self.c:
+                copy.wait_recv()
+            for copy in self.c:
+                copy.wait_send()
+
+    attn_gather, ffn_gather = Gather(attn_w, aw), Gather(ffn_w, fw)
+    vec_copies = [send(vec_w, vec_all.at[fs], (dp, (fs + i) % (2 * N_X))) for i in range(1, 2 * N_X)]
+    attn_gather.start()
+    vec_all[fs] = vec_w[...]
+    attn_gather.forward()
+    ffn_gather.start()
+    attn_gather.spread()
+    for copy in vec_copies:
+        copy.wait_recv()
+    for copy in vec_copies:
+        copy.wait_send()
+    pair_rows = 19
+    for i in range(N_X * pair_rows):
+        p, r = i // pair_rows, i % pair_rows
+        if r < 9:
+            row = vec_all[2 * p, r:r + 1, :]
+        elif r == 9:
+            row = vec_all[2 * p, 9:10, :] + vec_all[2 * p + 1, 0:1, :]
+        else:
+            row = vec_all[2 * p + 1, r - 9:r - 8, :]
+        vec[i // 4:i // 4 + 1, i % 4 * 128:i % 4 * 128 + 128] = row
+    attn_gather.finish()
+
+    ffn_reduce = Reduce(gf, lambda i: ga.at[i // 2, i % 2], ffn_out)
+    attn_reduce = Reduce(ga, lambda i: gp.at[i, 0:d_model], attn_out)
+    vec_reduce = ReduceVec()
 
     def rows(r):
         return pl.ds(pl.multiple_of(r * ROWS, ROWS), ROWS)
@@ -96,7 +380,7 @@
             return 0
         lax.fori_loop(0, n_batch * n_pairs, step, 0)
 
-    def attn_grad(q, k, v, do, causal):
+    def attn_grad(q, k, v, do, causal, part):
         def step(i, _):
             b = i // n_pairs
             hp = i % n_pairs
@@ -117,9 +401,11 @@
             k[s, c] = jnp.concatenate(dkt, axis=0).astype(BF).T
             v[s, c] = jnp.concatenate(dvt, axis=0).astype(BF).T
             return 0
-        lax.fori_loop(0, n_batch * n_pairs, step, 0)
+        half_steps = n_batch * n_pairs // 2
+        lax.fori_loop(part * half_steps, (part + 1) * half_steps, step, 0)
 
     attn(q, k, v, o, True)
+    ffn_gather.forward()
 
     def post_self(r, _):
         s = rows(r)
@@ -131,6 +417,8 @@
 
     lax.fori_loop(0, n_chunks, post_self, 0)
     attn(qc, kc, vc, oc, False)
+    ffn_gather.spread()
+    ffn_gather.finish()
 
     def ffn(r, _):
         s = rows(r)
@@ -160,7 +448,7 @@
     lax.fori_loop(0, n_chunks, ffn, 0)
 
     def ffn_grad(f, _):
-        gf[n_ffn + f] = mm_tn(g[f], dresb[...])
+        gf[(n_ffn + f) // 2, (n_ffn + f) % 2] = mm_tn(g[f], dresb[...])
 
         def up_grad(r, _):
             s = rows(r)
@@ -172,10 +460,11 @@
             return 0
 
         lax.fori_loop(0, n_chunks, up_grad, 0)
-        gf[f] = mm_tn(g[f], h2[...])
+        gf[f // 2, f % 2] = mm_tn(g[f], h2[...])
         return 0
 
     lax.fori_loop(0, n_ffn, ffn_grad, 0)
+    ffn_reduce.r0()
 
     def norm2_grad(r, _):
         s = rows(r)
@@ -188,11 +477,14 @@
         return 0
 
     lax.fori_loop(0, n_chunks, norm2_grad, 0)
-    ga[7] = mm_tn(oc[...], dresb[...])
-    attn_grad(qc, kc, vc, h2, False)
-    ga[4] = mm_tn(h1[...], qc[...])
-    ga[5] = mm_tn(enc[...], kc[...])
-    ga[6] = mm_tn(enc[...], vc[...])
+    ga[3, 1] = mm_tn(oc[...], dresb[...])
+    attn_grad(qc, kc, vc, h2, False, 0)
+    ffn_reduce.r1()
+    attn_grad(qc, kc, vc, h2, False, 1)
+    ffn_reduce.r2()
+    ga[2, 0] = mm_tn(h1[...], qc[...])
+    ga[2, 1] = mm_tn(enc[...], kc[...])
+    ga[3, 0] = mm_tn(enc[...], vc[...])
 
     def norm1_grad(r, _):
         s = rows(r)
@@ -209,11 +501,16 @@
         return 0
 
     lax.fori_loop(0, n_chunks, norm1_grad, 0)
-    ga[3] = mm_tn(o[...], dresb[...])
-    attn_grad(q, k, v, h2, True)
-    ga[0] = mm_tn(x[...], q[...])
-    ga[1] = mm_tn(x[...], k[...])
-    ga[2] = mm_tn(x[...], v[...])
+    ga[1, 1] = mm_tn(o[...], dresb[...])
+    attn_grad(q, k, v, h2, True, 0)
+    ffn_reduce.r3()
+    attn_grad(q, k, v, h2, True, 1)
+    ffn_reduce.r4()
+    ga[0, 0] = mm_tn(x[...], q[...])
+    ga[0, 1] = mm_tn(x[...], k[...])
+    ga[1, 0] = mm_tn(x[...], v[...])
+
+    attn_reduce.r0()
 
     def last(r, _):
         s = rows(r)
@@ -224,31 +521,27 @@
         return 0
 
     lax.fori_loop(0, n_chunks, last, 0)
-
-
-def local_layer(dec_in, enc_out, src_lens, tgt_lens, y_cot, aw, fw, vec):
-    n_batch, n_tgt, d = dec_in.shape
-    n_src = enc_out.shape[1]
-    n_tok = n_batch * n_tgt
-    ffn_dim = fw.shape[0] * d // 2
-    tok = lambda dt: pltpu.VMEM((n_tok, d), dt)
-    n_ffn = ffn_dim // d
-    vm = pl.BlockSpec(memory_space=pltpu.VMEM)
-    sm = pl.BlockSpec(memory_space=pltpu.SMEM)
-    act = jax.ShapeDtypeStruct((n_tok, d), BF)
-    col = pltpu.VMEM((n_tok, 1), F32)
-    y, dx, denc, ga, gf, gv = pl.pallas_call(
-        functools.partial(layer_kernel, n_batch, n_tgt, n_src, d, ffn_dim),
-        out_shape=(act, act, act, jax.ShapeDtypeStruct(aw.shape, F32), jax.ShapeDtypeStruct(fw.shape, F32), jax.ShapeDtypeStruct(vec.shape, F32)),
-        in_specs=[sm, sm] + [vm] * 6,
-        out_specs=(vm,) * 6,
-        scratch_shapes=[tok(BF)] * 4 + [tok(BF), tok(F32), col] + [tok(BF)] * 4 + [tok(F32), col, tok(BF),
-                        pltpu.VMEM((n_ffn, n_tok, d), F32), pltpu.VMEM((n_ffn, n_tok, d), BF), tok(F32), tok(F32), tok(BF)],
-        compiler_params=pltpu.CompilerParams(vmem_limit_bytes=67043328),
-        cost_estimate=pl.CostEstimate(flops=24 * 10**9, bytes_accessed=30 * 2**20, transcendentals=0),
-        name='layer',
-    )(src_lens, tgt_lens, dec_in.reshape(n_tok, d), enc_out.reshape(n_tok, d), y_cot.reshape(n_tok, d), aw, fw, vec)
-    return y.reshape(dec_in.shape), dx.reshape(dec_in.shape), denc.reshape(enc_out.shape), ga, gf, gv
+    ffn_reduce.r5()
+    attn_reduce.r1()
+    vec_reduce.r1()
+    ffn_reduce.r6()
+    vec_reduce.r2()
+    attn_reduce.r2()
+    vec_reduce.r3()
+    attn_reduce.r3()
+    attn_reduce.r4()
+    vec_reduce.r5()
+    ffn_reduce.r7()
+    attn_reduce.r5()
+    vec_reduce.r6()
+    attn_reduce.r6()
+    ffn_reduce.r8()
+    vec_reduce.r7()
+    attn_reduce.r7()
+    ffn_reduce.r9()
+    attn_reduce.r8()
+    attn_reduce.r9()
+    assert sem_count[0] <= send_sems.shape[0]
 
 
 def solution(mesh):
@@ -261,21 +554,41 @@
     vec_spec = P('fsdp')
 
     def device_step(dec_in, enc_out, src_lens, tgt_lens, y_cot, attn_w, ffn_w, vec_params):
-        d = attn_w.shape[1]
+        n_batch, n_tgt, d = dec_in.shape
+        n_src = enc_out.shape[1]
+        n_tok = n_batch * n_tgt
         n_vec = vec_params.shape[0]
-        vec_rows = -(-n_vec // d)
-        vec_pad = jnp.pad(vec_params, (0, vec_rows * d - n_vec)).reshape(vec_rows, d)
-        packed = lax.all_gather(jnp.concatenate([attn_w, vec_pad], axis=0), 'fsdp', axis=0)
-        aw = packed[:, :d]
-        vec = packed[:, d:].reshape(n_fsdp, vec_rows * d)[:, :n_vec].reshape(-1, d).astype(F32)
-        fw = lax.all_gather(ffn_w, 'fsdp', axis=0)
-        y, dx, denc, ga, gf, gv = local_layer(dec_in, enc_out, src_lens, tgt_lens, y_cot, aw, fw, vec)
-        scale = 1.0 / (dec_in.shape[0] * dec_in.shape[1] * n_fsdp * n_dp)
-        gv = lax.psum(gv.reshape(n_fsdp, n_vec), batch_axes)
-        gv = lax.dynamic_index_in_dim(gv, lax.axis_index('fsdp'), 0, keepdims=False)
-        ga = lax.psum_scatter(ga.reshape(-1, d), 'fsdp', scatter_dimension=0, tiled=True)
-        gf = lax.psum_scatter(gf.reshape(-1, d), 'fsdp', scatter_dimension=0, tiled=True)
-        ga, gf = lax.psum((ga, gf), 'dp')
-        return y, dx, denc, ga * scale, gf * scale, gv * scale
+        ffn_dim = n_fsdp * ffn_w.shape[0] // 2
+        n_ffn = ffn_dim // d
+        scale = 1.0 / (n_tok * n_fsdp * n_dp)
+        fs = lax.axis_index('fsdp')
+        vec_f = vec_params.astype(F32)
+        vec_w = jnp.where(fs % 2 == 0, jnp.pad(vec_f, (0, 2048 - n_vec)), jnp.pad(vec_f, (64, 2048 - 64 - n_vec))).reshape(16, 128)
+        vm = pl.BlockSpec(memory_space=pltpu.VMEM)
+        sm = pl.BlockSpec(memory_space=pltpu.SMEM)
+        act = jax.ShapeDtypeStruct((n_tok, d), BF)
+        block = jax.ShapeDtypeStruct((d, d), F32)
+        buf = lambda *shape: pltpu.VMEM(shape, F32)
+        tok = lambda dt: pltpu.VMEM((n_tok, d), dt)
+        col = pltpu.VMEM((n_tok, 1), F32)
+        weights = pltpu.VMEM((n_fsdp, d, d), BF)
+        y, dx, denc, ga, gf, gv = pl.pallas_call(
+            functools.partial(layer_kernel, n_batch, n_tgt, n_src, d, ffn_dim, scale),
+            out_shape=(act, act, act, block, block, jax.ShapeDtypeStruct((128, 128), F32)),
+            in_specs=[sm, sm] + [vm] * 6,
+            out_specs=(vm,) * 6,
+            scratch_shapes=[weights, weights, buf(N_X, 2, d, d), buf(N_X, 2, d, d), buf(32, d), buf(24, d), buf(n_fsdp, 16, 128)]
+            + [tok(BF)] * 4 + [tok(BF), tok(F32), col] + [tok(BF)] * 4 + [tok(F32), col, tok(BF)]
+            + [buf(n_ffn, n_tok, d), pltpu.VMEM((n_ffn, n_tok, d), BF), tok(F32), tok(BF)]
+            + [buf(2, 128, d), buf(2, 256, d), buf(2, 4, 32, d), buf(2, 4, 64, d), buf(2, 32, d), buf(2, 64, d), buf(2, 32, d), buf(2, 64, d)]
+            + [buf(7, 2, 8, d), buf(2, 128, 128), buf(4, 128, 128), buf(4, 128, 128), buf(7, 16, 128)]
+            + [pltpu.SemaphoreType.DMA((160,)), pltpu.SemaphoreType.DMA((160,))],
+            compiler_params=pltpu.CompilerParams(vmem_limit_bytes=67043328, collective_id=0, has_side_effects=True),
+            cost_estimate=pl.CostEstimate(flops=24 * 10**9, bytes_accessed=30 * 2**20, transcendentals=0),
+            name='layer',
+        )(src_lens, tgt_lens, dec_in.reshape(n_tok, d), enc_out.reshape(n_tok, d), y_cot.reshape(n_tok, d), attn_w, ffn_w, vec_w)
+        gv = gv.reshape(d // 128, 32, 128).transpose(1, 0, 2).reshape(-1)
+        gv = lax.dynamic_slice_in_dim(gv, fs * n_vec, n_vec)
+        return y.reshape(dec_in.shape), dx.reshape(dec_in.shape), denc.reshape(enc_out.shape), ga, gf, gv
 
     return jax.shard_map(device_step, mesh=mesh, in_specs=(act_spec, act_spec, len_spec, len_spec, act_spec, row_spec, row_spec, vec_spec), out_specs=(act_spec, act_spec, act_spec, row_spec, row_spec, vec_spec), check_vma=False)

time: 451 us -> 205 us (0.45)
  waiting for transfers between devices: 260 us -> 0 us
  Pallas kernels: 86.5 us -> 194 us
  blocking collectives: 76.1 us -> 0 us
  between operations: 13.8 us -> 0.67 us
  other arithmetic: 5.6 us -> 0.68 us
    reduce_scatter x2 -> x0, waiting for transfers between devices: 112 us -> none  [the longest x1 57.2 us: device_step(): lax.psum_scatter(gf.reshape(-1, d), 'fsdp', scatter_dimension=0, tiled=True)]
    pallas_call x1, Pallas kernels: 86.5 us -> 194 us  [device_step(): pl.pallas_call(functools.partial(layer_kernel, n_batch, n_tgt, n_src, d,...]
    psum x1 -> x0, waiting for transfers between devices: 79.6 us -> none  [device_step(): ga, gf = lax.psum((ga, gf), 'dp')]
    psum x1 -> x0, blocking collectives: 76.1 us -> none  [device_step(): gv = lax.psum(gv.reshape(n_fsdp, n_vec), batch_axes)]
    all_gather x2 -> x0, waiting for transfers between devices: 67.5 us -> none  [the longest x1 37.1 us: device_step(): lax.all_gather(jnp.concatenate([attn_w, vec_pad], axis=0), 'fsdp', axis=0)]
    unnamed x4 -> x15, local copies, waits for them, and re-layouts: 0.87 us -> 8.31 us
  transfers between devices with their start and end apart: 5 -> 0, of which waited for: 5 -> 0; matrix products, arithmetic and copies ran while one was open for 1% -> 0% of each run, Pallas kernels for 0% -> 0%
where the time goes in v2:
time: 205 us
  Pallas kernels  194 us (95%)
  local copies, waits for them, and re-layouts  9.88 us (5%)
    pallas_call x1, Pallas kernels, device_step(): pl.pallas_call(functools.partial(layer_kernel, n_batch, n_tgt, n_src, d,...  194 us
    unnamed x15, local copies, waits for them, and re-layouts  8.31 us

profile of v2, /device:TPU:8, one launch (start us, length us, event | category | flops | bytes accessed | tf_op | source)
XLA Modules:
  0.0 205.0 jit_solution(9090462574899705541)
XLA Ops:
  0.6 0.0 copy-start.4
  0.7 0.7 copy-done.4
  1.3 0.7 select_bitcast_fusion.vec_w
  2.0 193.8 %layer.1 = (bf16[768,512]{1,0:T(8,128)(2,1)}, bf16[768,512]{1,0:T(8,128)(2,1)}, bf16[768,512]{1,0:T(8,128)(2,1)}, f32[512,512]{1,0:T(8,128)}, f32[512,512]{1,0:T(8,128)}, /*index=5*/f32[128,128]{1,0:T(8,128)}) custom-call(s32[2]{0:T(128)} %src_lens.1, s32[2]{0:T(128)} %tgt_lens.1, bf16[768,512]{1,0:T(8,128)(2,1)} %bitcast.17, bf16[768,512]{1,0:T(8,128)(2,1)} %bitcast.18, ...), custom_call_target="tpu_custom_call" | custom-call | flops 24000000000 | bytes 31457280 | tf_op jit(solution)/shard_map/layer/pallas_call | solution.py:575
  195.8 0.9 copy.14
  196.7 0.7 dynamic_slice.3
  197.4 0.0 copy-start.3
  197.4 2.1 %copy.20 = bf16[2,384,512]{2,1,0:T(8,128)(2,1)} copy(bf16[2,384,512]{2,1,0:T(8,128)(2,1)} %bitcast.14) | data formatting | bytes 1572864
  199.5 0.0 copy-done.3
  199.5 0.0 copy-start.2
  199.5 0.9 copy.21
  200.4 0.5 copy-done.2
  200.9 0.0 copy-start.1
  200.9 0.9 copy.22
  201.8 0.6 copy-done.1
  202.4 0.0 copy-start
  202.4 1.0 copy.23
  203.4 0.6 copy-done
  204.1 1.0 copy.24
  (1 shorter events, 0.0 us)
Async XLA Ops:
  0.6 0.7 copy-start.4
  197.4 2.1 %copy-start.3 = (bf16[768,512]{1,0:T(8,128)(2,1)S(1)}, bf16[768,512]{1,0:T(8,128)(2,1)}, u32[]{:S(2)}) copy-start(bf16[768,512]{1,0:T(8,128)(2,1)} %get-tuple-element.13) | copy-start | bytes 2359300
  199.5 1.4 copy-start.2
  200.9 1.5 copy-start.1
  202.4 1.6 copy-start

commit v3 on v2

--- a/solution.py
+++ b/solution.py
@@ -29,19 +29,23 @@
 N_Y = 4
 N_Z = 8
 MESH = pl.DeviceIdType.MESH
-
-
-def layer_kernel(n_batch, n_tgt, n_src, d_model, ffn_dim, scale, src_lens, tgt_lens, x, enc, dy, attn_w, ffn_w, vec_w,
-                 y, dx, denc, attn_out, ffn_out, vec_out,
+FFN_PLAN = ((True, 256), (False, 256))
+ATTN_PLAN = ((False, 128), (True, 128), (False, 128), (True, 128))
+
+
+def layer_kernel(n_batch, n_tgt, n_src, d_model, ffn_dim, scale, src_lens, tgt_lens, x_any, enc_any, dy_any, attn_w, ffn_w, vec_w,
+                 y_any, dx_any, denc_any, attn_out, ffn_out, vec_out,
+                 x, enc, dy, y, dx, denc, local_sems,
                  aw, fw, ga, gf, gv, vec, vec_all, q, k, v, o, h1, n1, i1, qc, kc, vc, oc, n2, i2, h2, gp, g, dres, dresb,
-                 a1, a2, b1, b2, c1, c2, e1, e2, z_in, vec_pair, vec_x, vec_y, vec_z, send_sems, recv_sems):
+                 a1, a2, c1, c2, z_x, b1, b2, e1, e2, z_y, vec_pair, vec_x, vec_y, vec_z, send_sems, recv_sems):
     acc = dres
     n_ffn = ffn_dim // d_model
     n_tok = n_batch * n_tgt
     n_chunks = n_tok // ROWS
     n_pairs = d_model // 128
     half_rows = d_model // 2
-    y_rows = half_rows // N_Y
+    y_rows = d_model // N_Y
+    x_bufs, y_bufs = (a1, a2, c1, c2, z_x), (b1, b2, e1, e2, z_y)
     z_rows = y_rows // N_Z
 
     dp = lax.axis_index('dp')
@@ -74,6 +78,10 @@
         copy.start()
         return copy
 
+    loads = [pltpu.make_async_copy(src, dst, local_sems.at[i]) for i, (src, dst) in enumerate(((x_any, x), (enc_any, enc), (dy_any, dy)))]
+    stores = [pltpu.make_async_copy(src, dst, local_sems.at[3 + i]) for i, (src, dst) in enumerate(((y, y_any), (dx, dx_any), (denc, denc_any)))]
+    for load in loads:
+        load.start()
     barrier = pltpu.get_barrier_semaphore()
     peers = [(dp, (fs + i) % (2 * N_X)) for i in range(1, 2 * N_X)]
     peers += [along_y(i) for i in range(1, N_Y)] + [along_z(i) for i in range(1, N_Z)]
@@ -90,151 +98,192 @@
             self.copies.append(send(src, src, device))
             return self.copies[-1]
 
+        def half(self, ref, j):
+            return ref.at[half_rows * j:half_rows * (j + 1)]
+
+        def slot(self, step, j):
+            return self.half(self.full.at[self.xs[step] * 2 + core], j)
+
         def start(self):
             mine = self.full.at[fs]
-            self.up = send(self.block, mine, along_x(1))
-            self.down = send(self.block, mine, along_x(3))
+            self.first = [send(self.half(self.block, j), self.half(mine, j), along_x(1 + 2 * j)) for j in range(2)]
+            self.second = [send(self.half(self.block, 1 - j), self.half(mine, 1 - j), along_x(1 + 2 * j)) for j in range(2)]
             self.across = send(self.block, mine, partner)
             self.full[fs] = self.block[...]
 
         def forward(self):
-            prev = self.full.at[self.xs[3] * 2 + core]
-            nxt = self.full.at[self.xs[1] * 2 + core]
-            self.up.wait_recv()
-            self.up2 = send(self.full.at[self.xs[3] * 2 + core, 0:half_rows], self.full.at[self.xs[3] * 2 + core, 0:half_rows], along_x(1))
-            self.down.wait_recv()
-            self.down2 = send(self.full.at[self.xs[1] * 2 + core, half_rows:], self.full.at[self.xs[1] * 2 + core, half_rows:], along_x(3))
-            self.go(prev, partner)
-            self.go(nxt, partner)
+            self.hop = []
+            for j, came in ((0, 3), (1, 1)):
+                self.first[j].wait_recv()
+                self.hop.append(send(self.slot(came, j), self.slot(came, j), along_x(1 + 2 * j)))
+                self.go(self.slot(came, j), partner)
+            for j, came in ((0, 3), (1, 1)):
+                self.second[j].wait_recv()
+                self.go(self.slot(came, 1 - j), partner)
 
         def spread(self):
-            self.up2.wait_recv()
-            self.go(self.full.at[self.xs[2] * 2 + core, 0:half_rows], partner)
-            self.down2.wait_recv()
-            self.go(self.full.at[self.xs[2] * 2 + core, half_rows:], partner)
+            for j in range(2):
+                self.hop[j].wait_recv()
+                self.go(self.slot(2, j), partner)
 
         def finish(self):
             self.across.wait_recv()
             for copy in self.copies:
                 copy.wait_recv()
-            for copy in self.copies + [self.up, self.down, self.across, self.up2, self.down2]:
+            for copy in self.copies + self.first + self.second + self.hop + [self.across]:
                 copy.wait_send()
 
     class Ring:
-        def __init__(self, along, pos, part, bufs, sems=None):
-            self.along, self.pos, self.part, self.bufs = along, pos, part, bufs
+        def __init__(self, along, pos, part, near, full):
+            self.along, self.pos, self.part, self.near, self.full = along, pos, part, near, full
+            self.far, self.nxt, self.prev = (pos + 2) % 4, (pos + 1) % 4, (pos + 3) % 4
 
         def start(self):
-            near, _ = self.bufs
-            far = (self.pos + 2) % 4
-            self.c = [send(self.part(far, 0), near.at[0], self.along(1)), send(self.part(far, 1), near.at[1], self.along(3))]
+            self.c = [send(self.part(self.far, 0), self.near(0), self.along(1)), send(self.part(self.far, 1), self.near(1), self.along(3))]
+
+        def direct(self):
+            self.c += [send(self.part(self.nxt, 1), self.full(0, 1), self.along(1)), send(self.part(self.prev, 0), self.full(1, 0), self.along(3))]
 
         def relay(self):
-            near, full = self.bufs
-            nxt, prev = (self.pos + 1) % 4, (self.pos + 3) % 4
-            self.c[0].wait_recv()
-            self.part(nxt, 0)[...] += near[0]
-            self.c[1].wait_recv()
-            self.part(prev, 1)[...] += near[1]
-            self.c += [send(self.part(nxt, None), full.at[0], self.along(1)), send(self.part(prev, None), full.at[1], self.along(3))]
+            for way, target in ((0, self.nxt), (1, self.prev)):
+                self.c[way].wait_recv()
+                self.part(target, way)[...] += self.near(way)[...]
+                self.c.append(send(self.part(target, way), self.full(way, way), self.along(1 + 2 * way)))
 
         def finish(self):
-            _, full = self.bufs
-            self.c[2].wait_recv()
-            self.c[3].wait_recv()
-            self.part(self.pos, None)[...] += full[0] + full[1]
+            for copy in self.c[2:]:
+                copy.wait_recv()
+            self.part(self.pos, None)[...] += self.full(0, None)[...] + self.full(1, None)[...]
             for copy in self.c:
                 copy.wait_send()
 
-    def piece(start, size, i, j):
+    def split(start, size, j):
         if j is None:
-            return pl.ds(pl.multiple_of(start + size * i, 8), size)
-        return pl.ds(pl.multiple_of(start + size * i + size // 2 * j, 8), size // 2)
+            return pl.ds(pl.multiple_of(start, 8), size)
+        return pl.ds(pl.multiple_of(start + size // 2 * j, 8), size // 2)
 
     class Reduce:
-        def __init__(self, grad, pair_in, out):
-            self.grad, self.pair_in, self.out = grad, pair_in, out
-            own = lambda i, rows: grad.at[i, core, rows]
-            self.first = [Ring(along_x, my_x, lambda i, j: own(i, slice(0, half_rows) if j is None else slice(half_rows // 2 * j, half_rows // 2 * (j + 1))), (a1, a2)),
-                          Ring(along_y, my_y, lambda i, j: grad.at[:, core, piece(half_rows, y_rows, i, j)], (b1, b2))]
-            self.second = [Ring(along_y, my_y, lambda i, j: own(my_x, piece(0, y_rows, i, j)), (c1, c2)),
-                           Ring(along_x, my_x, lambda i, j: own(i, piece(half_rows + y_rows * my_y, y_rows, 0, j)), (e1, e2))]
-
-        def z_part(self, ref, h, z):
-            return ref.at[pl.ds(pl.multiple_of(half_rows * h + y_rows * my_y + z_rows * z, 8), z_rows)]
-
-        def y_part(self, h, pos):
-            return self.out.at[pl.ds(pl.multiple_of(half_rows * h + y_rows * pos, 8), y_rows)]
+        def __init__(self, grad, pair_in, out, x_first, lane, width, spare):
+            self.out = out
+            self.cols = cols = slice(lane, lane + width)
+            self.lands = lands = slice(spare, spare + width)
+            self.block = grad.at[core, my_x]
+            bufs = x_bufs if x_first else y_bufs
+            self.z_in = bufs[4]
+            near_in = lambda k: (lambda way: bufs[k].at[way, ..., lands])
+            full_in = lambda k: (lambda way, j: bufs[k].at[(way,) + (slice(None),) * (len(bufs[k].shape) - 3) + (split(0, bufs[k].shape[-2], j), lands)])
+            if x_first:
+                part_of = lambda c: (lambda i, j: grad.at[c, i, split(0, d_model, j), cols])
+                first = (along_x, my_x)
+                self.second = Ring(along_y, my_y, lambda i, j: grad.at[core, my_x, split(y_rows * i, y_rows, j), cols], near_in(2), full_in(3))
+                self.pair_part = lambda i: pair_in(i, slice(0, d_model), cols)
+            else:
+                part_of = lambda c: (lambda i, j: grad.at[c, :, split(y_rows * i, y_rows, j), cols])
+                first = (along_y, my_y)
+                self.second = Ring(along_x, my_x, lambda i, j: grad.at[core, i, split(y_rows * my_y, y_rows, j), cols], near_in(2), full_in(3))
+                self.pair_part = lambda i: pair_in(slice(None), split(y_rows * i, y_rows, None), cols)
+            self.first = Ring(*first, part_of(core), near_in(0), full_in(1))
+            self.pair_src = part_of(other)
+            self.pair = {}
+
+        def rows_at(self, ref, start, size):
+            return ref.at[pl.ds(pl.multiple_of(start, 8), size), self.cols]
+
+        def z_part(self, ref, z):
+            return self.rows_at(ref, y_rows * my_y + z_rows * z, z_rows)
+
+        def y_part(self, pos, half=None):
+            return self.out.at[split(y_rows * pos, y_rows, half), self.cols]
+
+        def swap(self, name):
+            i = getattr(self.first, name)
+            self.pair[name] = send(self.pair_src(i, None), self.pair_part(i), partner)
+
+        def merge(self, name):
+            i = getattr(self.first, name)
+            self.pair[name].wait_recv()
+            self.first.part(i, None)[...] += self.pair_part(i)[...]
+
+        def r1(self):
+            self.merge('far')
+            self.first.start()
+
+        def r1b(self):
+            self.merge('nxt')
+            self.merge('prev')
+            self.first.direct()
+
+        def r2(self):
+            self.first.relay()
+            self.merge('pos')
+
+        def r3(self):
+            for copy in self.pair.values():
+                copy.wait_send()
+            self.first.finish()
+            self.second.start()
+            self.second.direct()
+
+        def r4(self):
+            self.second.relay()
+
+        def r5(self):
+            self.second.finish()
+            self.z = [send(self.z_part(self.block, (my_z + i) % N_Z), self.z_in.at[i - 1, :, self.lands], along_z(i)) for i in range(1, N_Z)]
+
+        def r6(self):
+            for copy in self.z:
+                copy.wait_recv()
+            total = self.z_part(self.block, my_z)[...]
+            for i in range(1, N_Z):
+                total += self.z_in[i - 1, :, self.lands]
+            self.z_part(self.out, my_z)[...] = total * scale
+            for copy in self.z:
+                copy.wait_send()
+            self.z = [send(self.z_part(self.out, my_z), self.z_part(self.out, my_z), along_z(i)) for i in range(1, N_Z)]
+
+        def r7(self):
+            for copy in self.z:
+                copy.wait_recv()
+            for copy in self.z:
+                copy.wait_send()
+            self.c = [send(self.y_part(my_y), self.y_part(my_y), along_y(i)) for i in (1, 3)]
+
+        def r8(self):
+            for way, pos in ((0, (my_y + 3) % N_Y), (1, (my_y + 1) % N_Y)):
+                self.c[way].wait_recv()
+                self.c.append(send(self.y_part(pos, way), self.y_part(pos, way), along_y(1 + 2 * way)))
+
+        def r9(self):
+            for copy in self.c[2:]:
+                copy.wait_recv()
+            for copy in self.c:
+                copy.wait_send()
+
+    class Group:
+        def __init__(self, parts):
+            self.parts = parts
 
         def r0(self):
-            self.pair = [send(self.grad.at[i, other], self.pair_in(i), partner) for i in range(N_X)]
-
-        def r1(self):
-            for i in range(N_X):
-                self.pair[i].wait_recv()
-
-                def add(j, _):
-                    s = pl.ds(pl.multiple_of(j * 128, 128), 128)
-                    self.grad[i, core, s] += self.pair_in(i)[s]
-                    return 0
-
-                lax.fori_loop(0, d_model // 128, add, 0)
-            for copy in self.pair:
-                copy.wait_send()
-            for ring in self.first:
-                ring.start()
-
-        def r2(self):
-            for ring in self.first:
-                ring.relay()
-
-        def r3(self):
-            for ring in self.first:
-                ring.finish()
-            for ring in self.second:
-                ring.start()
-
-        def r4(self):
-            for ring in self.second:
-                ring.relay()
-
-        def r5(self):
-            for ring in self.second:
-                ring.finish()
-            block = self.grad.at[my_x, core]
-            self.z = [(i, h, send(self.z_part(block, h, (my_z + i) % N_Z), z_in.at[i - 1, h], along_z(i))) for i in range(1, N_Z) for h in range(2)]
-
-        def r6(self):
-            for _, _, copy in self.z:
-                copy.wait_recv()
-            block = self.grad.at[my_x, core]
-            for h in range(2):
-                total = self.z_part(block, h, my_z)[...]
-                for i in range(1, N_Z):
-                    total += z_in[i - 1, h]
-                self.z_part(self.out, h, my_z)[...] = total * scale
-            for _, _, copy in self.z:
-                copy.wait_send()
-            self.z = [(i, h, send(self.z_part(self.out, h, my_z), self.z_part(self.out, h, my_z), along_z(i))) for i in range(1, N_Z) for h in range(2)]
-
-        def r7(self):
-            for _, _, copy in self.z:
-                copy.wait_recv()
-            for _, _, copy in self.z:
-                copy.wait_send()
-            self.c = [send(self.y_part(h, my_y), self.y_part(h, my_y), along_y(i)) for i in (1, 3) for h in range(2)]
-
-        def r8(self):
-            for copy in self.c:
-                copy.wait_recv()
-            self.c += [send(self.y_part(0, (my_y + 3) % N_Y), self.y_part(0, (my_y + 3) % N_Y), along_y(1)),
-                       send(self.y_part(1, (my_y + 1) % N_Y), self.y_part(1, (my_y + 1) % N_Y), along_y(3))]
-
-        def r9(self):
-            for copy in self.c[4:]:
-                copy.wait_recv()
-            for copy in self.c:
-                copy.wait_send()
+            for name in ('far', 'nxt', 'prev', 'pos'):
+                for part in self.parts:
+                    part.swap(name)
+
+        def __getattr__(self, name):
+            def call():
+                for part in self.parts:
+                    getattr(part, name)()
+            return call
+
+    def reduce_all(grad, pair_in, out, plan):
+        used = {True: 0, False: 0}
+        parts = []
+        lane = 0
+        for x_first, width in plan:
+            parts.append(Reduce(grad, pair_in, out, x_first, lane, width, used[x_first]))
+            used[x_first] += width
+            lane += width
+        return Group(parts)
 
     class ReduceVec:
         def __init__(self):
@@ -311,9 +360,11 @@
             row = vec_all[2 * p + 1, r - 9:r - 8, :]
         vec[i // 4:i // 4 + 1, i % 4 * 128:i % 4 * 128 + 128] = row
     attn_gather.finish()
-
-    ffn_reduce = Reduce(gf, lambda i: ga.at[i // 2, i % 2], ffn_out)
-    attn_reduce = Reduce(ga, lambda i: gp.at[i, 0:d_model], attn_out)
+    for load in loads:
+        load.wait()
+
+    ffn_reduce = reduce_all(gf, lambda i, r, c: ga.at[0, i, r, c], ffn_out, FFN_PLAN)
+    attn_reduce = reduce_all(ga, lambda i, r, c: gp.at[i, r, c], attn_out, ATTN_PLAN)
     vec_reduce = ReduceVec()
 
     def rows(r):
@@ -380,7 +431,7 @@
             return 0
         lax.fori_loop(0, n_batch * n_pairs, step, 0)
 
-    def attn_grad(q, k, v, do, causal, part):
+    def attn_grad(q, k, v, do, causal, begin, end):
         def step(i, _):
             b = i // n_pairs
             hp = i % n_pairs
@@ -401,8 +452,8 @@
             k[s, c] = jnp.concatenate(dkt, axis=0).astype(BF).T
             v[s, c] = jnp.concatenate(dvt, axis=0).astype(BF).T
             return 0
-        half_steps = n_batch * n_pairs // 2
-        lax.fori_loop(part * half_steps, (part + 1) * half_steps, step, 0)
+        steps = n_batch * n_pairs
+        lax.fori_loop(begin * steps // 4, end * steps // 4, step, 0)
 
     attn(q, k, v, o, True)
     ffn_gather.forward()
@@ -446,9 +497,10 @@
         return 0
 
     lax.fori_loop(0, n_chunks, ffn, 0)
+    stores[0].start()
 
     def ffn_grad(f, _):
-        gf[(n_ffn + f) // 2, (n_ffn + f) % 2] = mm_tn(g[f], dresb[...])
+        gf[(n_ffn + f) % 2, (n_ffn + f) // 2] = mm_tn(g[f], dresb[...])
 
         def up_grad(r, _):
             s = rows(r)
@@ -460,7 +512,7 @@
             return 0
 
         lax.fori_loop(0, n_chunks, up_grad, 0)
-        gf[f // 2, f % 2] = mm_tn(g[f], h2[...])
+        gf[f % 2, f // 2] = mm_tn(g[f], h2[...])
         return 0
 
     lax.fori_loop(0, n_ffn, ffn_grad, 0)
@@ -477,21 +529,18 @@
         return 0
 
     lax.fori_loop(0, n_chunks, norm2_grad, 0)
-    ga[3, 1] = mm_tn(oc[...], dresb[...])
-    attn_grad(qc, kc, vc, h2, False, 0)
+    ga[1, 3] = mm_tn(oc[...], dresb[...])
     ffn_reduce.r1()
-    attn_grad(qc, kc, vc, h2, False, 1)
+    ffn_reduce.r1b()
+    attn_grad(qc, kc, vc, h2, False, 0, 2)
     ffn_reduce.r2()
-    ga[2, 0] = mm_tn(h1[...], qc[...])
-    ga[2, 1] = mm_tn(enc[...], kc[...])
-    ga[3, 0] = mm_tn(enc[...], vc[...])
+    attn_grad(qc, kc, vc, h2, False, 2, 4)
+    ga[0, 2] = mm_tn(h1[...], qc[...])
+    ga[1, 2] = mm_tn(enc[...], kc[...])
+    ga[0, 3] = mm_tn(enc[...], vc[...])
 
     def norm1_grad(r, _):
         s = rows(r)
-        add_vec(4, qc[s, :].astype(F32))
-        add_vec(5, kc[s, :].astype(F32))
-        add_vec(6, vc[s, :].astype(F32))
-        denc[s, :] = (mm_nt(kc[s, :], aw[5]) + mm_nt(vc[s, :], aw[6])).astype(BF)
         d1 = norm_grad(dres[s, :] + mm_nt(qc[s, :], aw[4]), n1[s, :], i1[s, :], 9)
         add_vec(3, d1)
         dres[s, :] = d1
@@ -502,18 +551,27 @@
 
     lax.fori_loop(0, n_chunks, norm1_grad, 0)
     ga[1, 1] = mm_tn(o[...], dresb[...])
-    attn_grad(q, k, v, h2, True, 0)
+    attn_grad(q, k, v, h2, True, 0, 2)
     ffn_reduce.r3()
-    attn_grad(q, k, v, h2, True, 1)
+    attn_grad(q, k, v, h2, True, 2, 3)
     ffn_reduce.r4()
+    attn_grad(q, k, v, h2, True, 3, 4)
+    ffn_reduce.r5()
     ga[0, 0] = mm_tn(x[...], q[...])
-    ga[0, 1] = mm_tn(x[...], k[...])
-    ga[1, 0] = mm_tn(x[...], v[...])
+    ga[1, 0] = mm_tn(x[...], k[...])
+    ga[0, 1] = mm_tn(x[...], v[...])
 
     attn_reduce.r0()
+    ffn_reduce.r6()
+    attn_reduce.r1()
+    attn_reduce.r1b()
 
     def last(r, _):
         s = rows(r)
+        add_vec(4, qc[s, :].astype(F32))
+        add_vec(5, kc[s, :].astype(F32))
+        add_vec(6, vc[s, :].astype(F32))
+        denc[s, :] = (mm_nt(kc[s, :], aw[5]) + mm_nt(vc[s, :], aw[6])).astype(BF)
         add_vec(0, q[s, :].astype(F32))
         add_vec(1, k[s, :].astype(F32))
         add_vec(2, v[s, :].astype(F32))
@@ -521,27 +579,33 @@
         return 0
 
     lax.fori_loop(0, n_chunks, last, 0)
-    ffn_reduce.r5()
-    attn_reduce.r1()
+    stores[1].start()
+    stores[2].start()
     vec_reduce.r1()
-    ffn_reduce.r6()
+    ffn_reduce.r7()
+    attn_reduce.r2()
     vec_reduce.r2()
-    attn_reduce.r2()
+    attn_reduce.r3()
     vec_reduce.r3()
-    attn_reduce.r3()
+    ffn_reduce.r8()
     attn_reduce.r4()
     vec_reduce.r5()
-    ffn_reduce.r7()
     attn_reduce.r5()
+    attn_reduce.r6()
     vec_reduce.r6()
-    attn_reduce.r6()
-    ffn_reduce.r8()
+    attn_reduce.r7()
     vec_reduce.r7()
-    attn_reduce.r7()
     ffn_reduce.r9()
     attn_reduce.r8()
     attn_reduce.r9()
+    for store in stores:
+        store.wait()
     assert sem_count[0] <= send_sems.shape[0]
+
+
+def copy_out(*refs):
+    for src, dst in zip(refs[:5], refs[5:]):
+        dst[...] = src[...]
 
 
 def solution(mesh):
@@ -565,6 +629,7 @@
         vec_f = vec_params.astype(F32)
         vec_w = jnp.where(fs % 2 == 0, jnp.pad(vec_f, (0, 2048 - n_vec)), jnp.pad(vec_f, (64, 2048 - 64 - n_vec))).reshape(16, 128)
         vm = pl.BlockSpec(memory_space=pltpu.VMEM)
+        hbm = pl.BlockSpec(memory_space=pl.ANY)
         sm = pl.BlockSpec(memory_space=pltpu.SMEM)
         act = jax.ShapeDtypeStruct((n_tok, d), BF)
         block = jax.ShapeDtypeStruct((d, d), F32)
@@ -575,18 +640,30 @@
         y, dx, denc, ga, gf, gv = pl.pallas_call(
             functools.partial(layer_kernel, n_batch, n_tgt, n_src, d, ffn_dim, scale),
             out_shape=(act, act, act, block, block, jax.ShapeDtypeStruct((128, 128), F32)),
-            in_specs=[sm, sm] + [vm] * 6,
-            out_specs=(vm,) * 6,
-            scratch_shapes=[weights, weights, buf(N_X, 2, d, d), buf(N_X, 2, d, d), buf(32, d), buf(24, d), buf(n_fsdp, 16, 128)]
+            in_specs=[sm, sm] + [hbm] * 3 + [vm] * 3,
+            out_specs=(hbm,) * 3 + (vm,) * 3,
+            scratch_shapes=[tok(BF)] * 6 + [pltpu.SemaphoreType.DMA((6,)), weights, weights, buf(2, N_X, d, d), buf(2, N_X, d, d), buf(32, d), buf(24, d), buf(n_fsdp, 16, 128)]
             + [tok(BF)] * 4 + [tok(BF), tok(F32), col] + [tok(BF)] * 4 + [tok(F32), col, tok(BF)]
             + [buf(n_ffn, n_tok, d), pltpu.VMEM((n_ffn, n_tok, d), BF), tok(F32), tok(BF)]
-            + [buf(2, 128, d), buf(2, 256, d), buf(2, 4, 32, d), buf(2, 4, 64, d), buf(2, 32, d), buf(2, 64, d), buf(2, 32, d), buf(2, 64, d)]
-            + [buf(7, 2, 8, d), buf(2, 128, 128), buf(4, 128, 128), buf(4, 128, 128), buf(7, 16, 128)]
-            + [pltpu.SemaphoreType.DMA((160,)), pltpu.SemaphoreType.DMA((160,))],
+            + [buf(2, d // 2, 256), buf(2, d, 256), buf(2, 64, 256), buf(2, 128, 256), buf(7, 16, 256)]
+            + [buf(2, N_X, 64, 256), buf(2, N_X, 128, 256), buf(2, 64, 256), buf(2, 128, 256), buf(7, 16, 256)]
+            + [buf(2, 128, 128), buf(4, 128, 128), buf(4, 128, 128), buf(7, 16, 128)]
+            + [pltpu.SemaphoreType.DMA((260,)), pltpu.SemaphoreType.DMA((260,))],
             compiler_params=pltpu.CompilerParams(vmem_limit_bytes=67043328, collective_id=0, has_side_effects=True),
             cost_estimate=pl.CostEstimate(flops=24 * 10**9, bytes_accessed=30 * 2**20, transcendentals=0),
             name='layer',
         )(src_lens, tgt_lens, dec_in.reshape(n_tok, d), enc_out.reshape(n_tok, d), y_cot.reshape(n_tok, d), attn_w, ffn_w, vec_w)
+        n_steps = 4
+        tiles = [pl.BlockSpec((arr.shape[0] // n_steps, d), lambda i: (i, 0)) for arr in (y, dx, denc, ga, gf)]
+        y, dx, denc, ga, gf = pl.pallas_call(
+            copy_out,
+            grid=(n_steps,),
+            out_shape=tuple(jax.ShapeDtypeStruct(arr.shape, arr.dtype) for arr in (y, dx, denc, ga, gf)),
+            in_specs=tiles,
+            out_specs=tuple(tiles),
+            compiler_params=pltpu.CompilerParams(vmem_limit_bytes=67043328),
+            name='out',
+        )(y, dx, denc, ga, gf)
         gv = gv.reshape(d // 128, 32, 128).transpose(1, 0, 2).reshape(-1)
         gv = lax.dynamic_slice_in_dim(gv, fs * n_vec, n_vec)
         return y.reshape(dec_in.shape), dx.reshape(dec_in.shape), denc.reshape(enc_out.shape), ga, gf, gv

time: 205 us -> 190 us (0.927)
  Pallas kernels: 194 us -> 186 us
  local copies, waits for them, and re-layouts: 9.88 us -> 2.24 us
    pallas_call x1, Pallas kernels: 194 us -> 181 us  [device_step(): pl.pallas_call(functools.partial(layer_kernel, n_batch, n_tgt, n_src, d,...]
    unnamed x15 -> x2, local copies, waits for them, and re-layouts: 8.31 us -> 0.68 us
    pallas_call x0 -> x1, Pallas kernels: none -> 4.89 us  [device_step(): pl.pallas_call(copy_out, grid=(n_steps,), out_shape=tuple((jax.ShapeDtype...]
where the time goes in v3:
time: 190 us
  Pallas kernels  186 us (98%)
  local copies, waits for them, and re-layouts  2.24 us (1%)
    pallas_call x1, Pallas kernels, device_step(): pl.pallas_call(functools.partial(layer_kernel, n_batch, n_tgt, n_src, d,...  181 us
    pallas_call x1, Pallas kernels, device_step(): pl.pallas_call(copy_out, grid=(n_steps,), out_shape=tuple((jax.ShapeDtype...  4.89 us

profile of v3, /device:TPU:8, one launch (start us, length us, event | category | flops | bytes accessed | tf_op | source)
XLA Modules:
  0.0 189.6 jit_solution(1441612058828878966)
XLA Ops:
  0.6 0.0 copy-start
  0.7 0.7 copy-done
  1.3 0.7 select_bitcast_fusion.vec_w
  2.0 181.1 %layer.1 = (bf16[768,512]{1,0:T(8,128)(2,1)}, bf16[768,512]{1,0:T(8,128)(2,1)}, bf16[768,512]{1,0:T(8,128)(2,1)}, f32[512,512]{1,0:T(8,128)}, f32[512,512]{1,0:T(8,128)}, /*index=5*/f32[128,128]{1,0:T(8,128)}) custom-call(s32[2]{0:T(128)} %src_lens.1, s32[2]{0:T(128)} %tgt_lens.1, bf16[768,512]{1,0:T(8,128)(2,1)} %bitcast.14, bf16[768,512]{1,0:T(8,128)(2,1)} %bitcast.15, ...), custom_call_target="tpu_custom_call" | custom-call | flops 24000000000 | bytes 31457280 | tf_op jit(solution)/shard_map/layer/pallas_call | solution.py:640
  183.1 4.9 %out.1 = (bf16[768,512]{1,0:T(8,128)(2,1)}, bf16[768,512]{1,0:T(8,128)(2,1)}, bf16[768,512]{1,0:T(8,128)(2,1)}, f32[512,512]{1,0:T(8,128)}, f32[512,512]{1,0:T(8,128)}) custom-call(bf16[768,512]{1,0:T(8,128)(2,1)} %get-tuple-element.17.refs_0_, bf16[768,512]{1,0:T(8,128)(2,1)} %get-tuple-element.18.refs_1_, bf16[768,512]{1,0:T(8,128)(2,1)} %get-tuple-element.19.refs_2_, ...), custom_call_target="tpu_custom_call" | custom-call | tf_op jit(solution)/shard_map/out/pallas_call | solution.py:658
  188.0 0.9 copy.14
  188.9 0.7 dynamic_slice.3
  (1 shorter events, 0.0 us)
Async XLA Ops:
  0.6 0.7 copy-start

commit v4 on v3

--- a/solution.py
+++ b/solution.py
@@ -10,7 +10,7 @@
 MASK_FILL = -1e30
 BF = jnp.bfloat16
 F32 = jnp.float32
-ROWS = 256
+ROWS = 768
 
 
 def mm(a, b):
@@ -29,16 +29,17 @@
 N_Y = 4
 N_Z = 8
 MESH = pl.DeviceIdType.MESH
+ALL = slice(None)
 FFN_PLAN = ((True, 256), (False, 256))
 ATTN_PLAN = ((False, 128), (True, 128), (False, 128), (True, 128))
 
 
 def layer_kernel(n_batch, n_tgt, n_src, d_model, ffn_dim, scale, src_lens, tgt_lens, x_any, enc_any, dy_any, attn_w, ffn_w, vec_w,
                  y_any, dx_any, denc_any, attn_out, ffn_out, vec_out,
-                 x, enc, dy, y, dx, denc, local_sems,
+                 x, enc, dy, y, denc, local_sems,
                  aw, fw, ga, gf, gv, vec, vec_all, q, k, v, o, h1, n1, i1, qc, kc, vc, oc, n2, i2, h2, gp, g, dres, dresb,
                  a1, a2, c1, c2, z_x, b1, b2, e1, e2, z_y, vec_pair, vec_x, vec_y, vec_z, send_sems, recv_sems):
-    acc = dres
+    acc, dx = dres, dy
     n_ffn = ffn_dim // d_model
     n_tok = n_batch * n_tgt
     n_chunks = n_tok // ROWS
@@ -171,7 +172,7 @@
             bufs = x_bufs if x_first else y_bufs
             self.z_in = bufs[4]
             near_in = lambda k: (lambda way: bufs[k].at[way, ..., lands])
-            full_in = lambda k: (lambda way, j: bufs[k].at[(way,) + (slice(None),) * (len(bufs[k].shape) - 3) + (split(0, bufs[k].shape[-2], j), lands)])
+            full_in = lambda k: (lambda way, j: bufs[k].at[(way,) + (ALL,) * (len(bufs[k].shape) - 3) + (split(0, bufs[k].shape[-2], j), lands)])
             if x_first:
                 part_of = lambda c: (lambda i, j: grad.at[c, i, split(0, d_model, j), cols])
                 first = (along_x, my_x)
@@ -181,7 +182,7 @@
                 part_of = lambda c: (lambda i, j: grad.at[c, :, split(y_rows * i, y_rows, j), cols])
                 first = (along_y, my_y)
                 self.second = Ring(along_x, my_x, lambda i, j: grad.at[core, i, split(y_rows * my_y, y_rows, j), cols], near_in(2), full_in(3))
-                self.pair_part = lambda i: pair_in(slice(None), split(y_rows * i, y_rows, None), cols)
+                self.pair_part = lambda i: pair_in(ALL, split(y_rows * i, y_rows, None), cols)
             self.first = Ring(*first, part_of(core), near_in(0), full_in(1))
             self.pair_src = part_of(other)
             self.pair = {}
@@ -407,6 +408,9 @@
     def half(val, j):
         return jnp.where(low_half if j == 0 else ~low_half, val, jnp.zeros_like(val))
 
+    def both(val):
+        return jnp.concatenate([half(val, 0), half(val, 1)], axis=0)
+
     def key_mask(b, causal):
         key_pos = lax.broadcasted_iota(jnp.int32, (n_tgt, n_src), 1)
         if causal:
@@ -426,8 +430,9 @@
             c = pl.ds(pl.multiple_of(hp * 128, 128), 128)
             q2, k2, v2 = q[s, c], k[s, c], v[s, c]
             mask = key_mask(b, causal)
-            outs = [mm(prob(half(q2, j), k2, mask).astype(BF), v2) for j in range(2)]
-            o[s, c] = jnp.where(low_half, outs[0], outs[1]).astype(BF)
+            mask = jnp.concatenate([mask, mask], axis=0)
+            outs = mm(prob(both(q2), k2, mask).astype(BF), v2)
+            o[s, c] = jnp.where(low_half, outs[:n_tgt], outs[n_tgt:]).astype(BF)
             return 0
         lax.fori_loop(0, n_batch * n_pairs, step, 0)
 
@@ -440,15 +445,14 @@
             q2, k2, v2, do2 = q[s, c], k[s, c], v[s, c], do[s, c]
             mask = key_mask(b, causal)
             qt, dot = q2.T, do2.T
-            dq, dkt, dvt = [], [], []
-            for j in range(2):
-                p = prob(half(q2, j), k2, mask)
-                dp = mm_nt(half(do2, j), v2)
-                dvt.append(mm(dot[64 * j:64 * j + 64], p.astype(BF)))
-                ds = (p * (dp - jnp.sum(p * dp, axis=-1, keepdims=True))).astype(BF)
-                dq.append(mm(ds, k2))
-                dkt.append(mm(qt[64 * j:64 * j + 64], ds))
-            q[s, c] = (jnp.where(low_half, dq[0], dq[1]) * 0.125).astype(BF)
+            p = prob(both(q2), k2, jnp.concatenate([mask, mask], axis=0))
+            dp = mm_nt(both(do2), v2)
+            ds = (p * (dp - jnp.sum(p * dp, axis=-1, keepdims=True))).astype(BF)
+            pb = p.astype(BF)
+            dq = mm(ds, k2)
+            dvt = [mm(dot[64 * j:64 * j + 64], pb[n_tgt * j:n_tgt * (j + 1)]) for j in range(2)]
+            dkt = [mm(qt[64 * j:64 * j + 64], ds[n_tgt * j:n_tgt * (j + 1)]) for j in range(2)]
+            q[s, c] = (jnp.where(low_half, dq[:n_tgt], dq[n_tgt:]) * 0.125).astype(BF)
             k[s, c] = jnp.concatenate(dkt, axis=0).astype(BF).T
             v[s, c] = jnp.concatenate(dvt, axis=0).astype(BF).T
             return 0
@@ -633,6 +637,7 @@
         sm = pl.BlockSpec(memory_space=pltpu.SMEM)
         act = jax.ShapeDtypeStruct((n_tok, d), BF)
         block = jax.ShapeDtypeStruct((d, d), F32)
+        half = d // 2
         buf = lambda *shape: pltpu.VMEM(shape, F32)
         tok = lambda dt: pltpu.VMEM((n_tok, d), dt)
         col = pltpu.VMEM((n_tok, 1), F32)
@@ -642,11 +647,11 @@
             out_shape=(act, act, act, block, block, jax.ShapeDtypeStruct((128, 128), F32)),
             in_specs=[sm, sm] + [hbm] * 3 + [vm] * 3,
             out_specs=(hbm,) * 3 + (vm,) * 3,
-            scratch_shapes=[tok(BF)] * 6 + [pltpu.SemaphoreType.DMA((6,)), weights, weights, buf(2, N_X, d, d), buf(2, N_X, d, d), buf(32, d), buf(24, d), buf(n_fsdp, 16, 128)]
+            scratch_shapes=[tok(BF)] * 5 + [pltpu.SemaphoreType.DMA((6,)), weights, weights, buf(2, N_X, d, d), buf(2, N_X, d, d), buf(32, d), buf(24, d), buf(n_fsdp, 16, 128)]
             + [tok(BF)] * 4 + [tok(BF), tok(F32), col] + [tok(BF)] * 4 + [tok(F32), col, tok(BF)]
             + [buf(n_ffn, n_tok, d), pltpu.VMEM((n_ffn, n_tok, d), BF), tok(F32), tok(BF)]
-            + [buf(2, d // 2, 256), buf(2, d, 256), buf(2, 64, 256), buf(2, 128, 256), buf(7, 16, 256)]
-            + [buf(2, N_X, 64, 256), buf(2, N_X, 128, 256), buf(2, 64, 256), buf(2, 128, 256), buf(7, 16, 256)]
+            + [buf(2, d // 2, half), buf(2, d, half), buf(2, 64, half), buf(2, 128, half), buf(7, 16, half)]
+            + [buf(2, N_X, 64, half), buf(2, N_X, 128, half), buf(2, 64, half), buf(2, 128, half), buf(7, 16, half)]
             + [buf(2, 128, 128), buf(4, 128, 128), buf(4, 128, 128), buf(7, 16, 128)]
             + [pltpu.SemaphoreType.DMA((260,)), pltpu.SemaphoreType.DMA((260,))],
             compiler_params=pltpu.CompilerParams(vmem_limit_bytes=67043328, collective_id=0, has_side_effects=True),

time: 190 us -> 173 us (0.911)
  Pallas kernels: 186 us -> 169 us
    pallas_call x1, Pallas kernels: 181 us -> 164 us  [device_step(): pl.pallas_call(functools.partial(layer_kernel, n_batch, n_tgt, n_src, d,...]
where the time goes in v4:
time: 173 us; the launch traced here: 172 us
  Pallas kernels  169 us (98%)
  local copies, waits for them, and re-layouts  2.24 us (1%)
    pallas_call x1, Pallas kernels, device_step(): pl.pallas_call(functools.partial(layer_kernel, n_batch, n_tgt, n_src, d,...  164 us
    pallas_call x1, Pallas kernels, device_step(): pl.pallas_call(copy_out, grid=(n_steps,), out_shape=tuple((jax.ShapeDtype...  4.89 us

profile of v4, /device:TPU:8, one launch (start us, length us, event | category | flops | bytes accessed | tf_op | source)
XLA Modules:
  0.0 172.4 jit_solution(17352944065975301688)
XLA Ops:
  0.6 0.0 copy-start
  0.7 0.7 copy-done
  1.3 0.7 select_bitcast_fusion.vec_w
  2.0 163.9 %layer.1 = (bf16[768,512]{1,0:T(8,128)(2,1)}, bf16[768,512]{1,0:T(8,128)(2,1)}, bf16[768,512]{1,0:T(8,128)(2,1)}, f32[512,512]{1,0:T(8,128)}, f32[512,512]{1,0:T(8,128)}, /*index=5*/f32[128,128]{1,0:T(8,128)}) custom-call(s32[2]{0:T(128)} %src_lens.1, s32[2]{0:T(128)} %tgt_lens.1, bf16[768,512]{1,0:T(8,128)(2,1)} %bitcast.14, bf16[768,512]{1,0:T(8,128)(2,1)} %bitcast.15, ...), custom_call_target="tpu_custom_call" | custom-call | flops 24000000000 | bytes 31457280 | tf_op jit(solution)/shard_map/layer/pallas_call | solution.py:645
  166.0 4.9 %out.1 = (bf16[768,512]{1,0:T(8,128)(2,1)}, bf16[768,512]{1,0:T(8,128)(2,1)}, bf16[768,512]{1,0:T(8,128)(2,1)}, f32[512,512]{1,0:T(8,128)}, f32[512,512]{1,0:T(8,128)}) custom-call(bf16[768,512]{1,0:T(8,128)(2,1)} %get-tuple-element.17.refs_0_, bf16[768,512]{1,0:T(8,128)(2,1)} %get-tuple-element.18.refs_1_, bf16[768,512]{1,0:T(8,128)(2,1)} %get-tuple-element.19.refs_2_, ...), custom_call_target="tpu_custom_call" | custom-call | tf_op jit(solution)/shard_map/out/pallas_call | solution.py:663
  170.8 0.9 copy.14
  171.7 0.7 dynamic_slice.3
  (1 shorter events, 0.0 us)
Async XLA Ops:
  0.6 0.7 copy-start
